TPU v7x, 32 devices: a 4x4x1 block of a 4x4x8 slice. The times are simulated.
32 devices in a mesh: part: 1 (over z), tp: 4 (over y), dp: 8 (over x, core).
Axes of the slice: x: 4, y: 4, z: 1, core: 2. Of those that a mesh axis runs over, the one named last changes fastest.
The devices are a block of a 4x4x8 slice.
Arguments:
- x: bfloat16 [2048, 5120], P(('part', 'dp', 'tp'))
- w_gate: bfloat16 [5120, 13824], P(('part', 'dp'), 'tp')
- w_up: bfloat16 [5120, 13824], P(('part', 'dp'), 'tp')
- w_down: bfloat16 [13824, 5120], P(('part', 'tp'), 'dp')
- dy: bfloat16 [2048, 5120], P(('part', 'dp', 'tp'))
Outputs:
- output 1: bfloat16 [2048, 5120], P(('part', 'dp', 'tp'))
- output 2: bfloat16 [2048, 5120], P(('part', 'dp', 'tp'))
- output 3: float32 [5120, 13824], P(('part', 'dp'), 'tp')
- output 4: float32 [5120, 13824], P(('part', 'dp'), 'tp')
- output 5: float32 [13824, 5120], P(('part', 'tp'), 'dp')
All inputs are finite; a program needn't handle non-finite values.
Results may differ from a plain program's by a relative error of at most 0.00104.
Values are sent between devices in bfloat16 or wider.
A program may use at most 768 MiB of HBM per device.

v0:
```python
import jax
import jax.numpy as jnp
from jax import lax
from jax.sharding import PartitionSpec as P


def solution(mesh):
    nx = mesh.shape['dp']
    ny = mesh.shape['tp']
    row_spec = P(('part', 'dp', 'tp'), None)
    win_spec = P(('part', 'dp'), 'tp')
    wout_spec = P(('part', 'tp'), 'dp')
    f32 = jnp.float32
    bf16 = jnp.bfloat16

    def to_cols(t):
        td, d = t.shape
        t = t.reshape(td, nx, d // nx).transpose(1, 0, 2)
        return lax.all_to_all(t, 'dp', 0, 0, tiled=True)

    def from_cols(u):
        v = lax.all_to_all(u, 'dp', 0, 0, tiled=True)
        return v.transpose(1, 0, 2).reshape(v.shape[1], -1)

    def f(x, wg, wu, wd, dy):
        td = x.shape[0]
        dc = wg.shape[0]
        fc = wg.shape[1]
        xd = to_cols(x)
        xs = lax.all_gather(xd, 'tp', axis=0, tiled=False)
        xs2 = xs.reshape(-1, dc)
        a_p = jnp.dot(xs2, wg, preferred_element_type=f32).reshape(ny, nx, td, fc)
        b_p = jnp.dot(xs2, wu, preferred_element_type=f32).reshape(ny, nx, td, fc)
        a = lax.psum_scatter(a_p.transpose(1, 0, 2, 3), 'dp', scatter_dimension=0, tiled=False).reshape(ny * td, fc)
        b = lax.psum_scatter(b_p.transpose(1, 0, 2, 3), 'dp', scatter_dimension=0, tiled=False).reshape(ny * td, fc)
        sig = jax.nn.sigmoid(a)
        act = a * sig
        h = (act * b).astype(bf16)
        h_all = lax.all_gather(h, 'dp', axis=0, tiled=False).reshape(nx, ny, td, fc)
        y_p = jnp.dot(h_all.reshape(-1, fc), wd, preferred_element_type=f32).reshape(nx, ny, td, dc)
        y_s = lax.psum_scatter(y_p.transpose(1, 0, 2, 3), 'tp', scatter_dimension=0, tiled=False)
        y = from_cols((xd.astype(f32) + y_s).astype(bf16))
        dyd = to_cols(dy)
        dys = lax.all_gather(dyd, 'tp', axis=0, tiled=False)
        g_p = jnp.einsum('nc,fc->nf', dys.reshape(-1, dc), wd, preferred_element_type=f32).reshape(ny, nx, td, fc)
        g = lax.psum_scatter(g_p.transpose(1, 0, 2, 3), 'dp', scatter_dimension=0, tiled=False).reshape(ny * td, fc)
        da = (g * b * sig * (1.0 + a * (1.0 - sig))).astype(bf16)
        db = (g * act).astype(bf16)
        dwd = jnp.einsum('kjtf,jktc->fc', h_all, dys, preferred_element_type=f32)
        da_all = lax.all_gather(da, 'dp', axis=0, tiled=False).reshape(nx, ny, td, fc)
        db_all = lax.all_gather(db, 'dp', axis=0, tiled=False).reshape(nx, ny, td, fc)
        dwg = jnp.einsum('jktc,kjtf->cf', xs, da_all, preferred_element_type=f32)
        dwu = jnp.einsum('jktc,kjtf->cf', xs, db_all, preferred_element_type=f32)
        dx_p = jnp.einsum('kjtf,cf->kjtc', da_all, wg, preferred_element_type=f32) + jnp.einsum('kjtf,cf->kjtc', db_all, wu, preferred_element_type=f32)
        dx_s = lax.psum_scatter(dx_p.transpose(1, 0, 2, 3), 'tp', scatter_dimension=0, tiled=False)
        dx = from_cols((dyd.astype(f32) + dx_s).astype(bf16))
        return y, dx, dwg, dwu, dwd

    return jax.shard_map(f, mesh=mesh, in_specs=(row_spec, win_spec, win_spec, wout_spec, row_spec), out_specs=(row_spec, row_spec, win_spec, win_spec, wout_spec), check_vma=False)
```

profile of v0, /device:TPU:97, one launch (start us, length us, event | category | flops | bytes accessed | tf_op | source)
XLA Modules:
  0.0 1446.0 jit_solution(10519287948770680628)
XLA Ops:
  7.2 0.1 all-gather.14.cloned.1.call-start
  7.3 1.2 copy.60
  8.5 0.1 copy.33
  8.6 16.7 %all_to_all.20 = bf16[8,64,640]{2,1,0:T(8,128)(2,1)} all-to-all(bf16[8,64,640]{2,1,0:T(8,128)(2,1)S(1)} %copy.33), channel_id=1, replica_groups=mesh['part'=1,'tp'=4,'dp'=8] {'dp'}, dimensions={0} | all-to-all | bytes 1310720 | tf_op jit(solution)/shard_map/all_to_all | solution.py:19
  25.2 0.1 all-gather.14.cloned.1.call-update
  25.3 0.1 all-gather.16.cloned.1.call-start
  25.4 0.1 copy.61
  25.5 0.1 copy.35
  25.6 14.8 %all_to_all.21 = bf16[8,64,640]{2,1,0:T(8,128)(2,1)} all-to-all(bf16[8,64,640]{2,1,0:T(8,128)(2,1)S(1)} %copy.35), channel_id=1, replica_groups=mesh['part'=1,'tp'=4,'dp'=8] {'dp'}, dimensions={0} | all-to-all | bytes 1310720 | tf_op jit(solution)/shard_map/all_to_all | solution.py:19
  40.3 0.1 all-gather.16.cloned.1.call-update
  40.4 0.1 all-reduce.10.cloned.1.call-start
  40.5 18.3 %all-gather.14.cloned.1.call-done = bf16[32,64,640]{2,1,0:T(8,128)(2,1)} async-done(((bf16[8,64,640]{2,1,0:T(8,128)(2,1)}), bf16[32,64,640]{2,1,0:T(8,128)(2,1)}) %all-gather.14.cloned.1.call-update) | async-done | bytes 2621456 | tf_op jit(solution)/shard_map/all_gather | solution.py:30
  58.8 19.6 %convolution_bitcast_fusion.1 = f32[8,4,64,3456]{3,2,0,1:T(8,128)} fusion(bf16[4,8,64,640]{3,2,1,0:T(8,128)(2,1)} %bitcast.147, bf16[640,3456]{1,0:T(8,128)(2,1)} %param.7), kind=kOutput, calls=%fused_computation.7 | convolution fusion | flops 9059696640 | bytes 35356672 | tf_op jit(solution)/shard_map/dot_general | solution.py:33
  78.4 15.0 %convolution_bitcast_fusion.2 = f32[8,4,64,3456]{3,2,0,1:T(8,128)} fusion(bf16[4,8,64,640]{3,2,1,0:T(8,128)(2,1)S(1)} %bitcast.148, bf16[640,3456]{1,0:T(8,128)(2,1)S(1)} %bitcast.144), kind=kOutput, calls=%fused_computation.8 | convolution fusion | flops 9059696640 | bytes 35356672 | tf_op jit(solution)/shard_map/dot_general | solution.py:32
  93.4 19.3 %convolution_bitcast_fusion = f32[8,4,64,3456]{3,2,0,1:T(8,128)} fusion(bf16[4,8,64,640]{3,2,1,0:T(8,128)(2,1)} %bitcast.145, bf16[3456,640]{1,0:T(8,128)(2,1)} %param.8), kind=kOutput, calls=%fused_computation.6 | convolution fusion | flops 9059696640 | bytes 35356672 | tf_op jit(solution)/shard_map/nc,fc->nf/dot_general | solution.py:45
  112.8 0.2 all-gather.12.cloned.1.call-start
  113.1 0.3 copy-done.5
  113.4 0.6 dynamic-slice
  114.0 816.2 %all-reduce.10.cloned.1.call-done = (f32[8,4,64,3456]{3,2,0,1:T(8,128)}, f32[8,4,64,3456]{3,2,0,1:T(8,128)}, f32[8,4,64,3456]{3,2,0,1:T(8,128)}) async-done(((f32[8,4,64,3456]{3,2,0,1:T(8,128)}, f32[8,4,64,3456]{3,2,0,1:T(8,128)}, f32[8,4,64,3456]{3,2,0,1:T(8,128)}), (f32[8,4,64,3456]{3,2,0,1:T(8,128)}, f32[8,4,64,3456]{3,2,0,1:T(8,128)}, f32[8,4,64,3456]{3,2,0,1:T(8,128)})) %all-reduce.10.cloned.1.call-update) | async-done | bytes 84934672
  930.2 2.9 constant_dynamic-slice_fusion.2
  933.1 4.2 constant_dynamic-slice_fusion
  937.4 3.6 multiply_convert_fusion.1
  941.0 0.1 all-gather.12.cloned.1.call-update
  941.0 0.1 all-gather.8.cloned.1.call-start
  941.1 0.6 all-gather.8.cloned.1.call-update
  941.7 0.1 all-gather.10.cloned.1.call-start
  941.8 0.6 all-gather.10.cloned.1.call-update
  942.3 0.1 all-reduce.12.cloned.1.call-start
  942.4 70.8 %all-gather.12.cloned.1.call-done = bf16[8,256,3456]{2,1,0:T(8,128)(2,1)} async-done(((bf16[1,256,3456]{2,1,0:T(8,128)(2,1)}), bf16[8,256,3456]{2,1,0:T(8,128)(2,1)}) %all-gather.12.cloned.1.call-update) | async-done | bytes 14155792 | tf_op jit(solution)/shard_map/all_gather | solution.py:51
  1013.2 17.5 %fusion.15 = f32[8,4,64,640]{3,2,1,0:T(8,128)} fusion(bf16[8,4,64,3456]{3,2,1,0:T(8,128)(2,1)} %bitcast.139, bf16[640,3456]{1,0:T(8,128)(2,1)} %param.7), kind=kOutput, calls=%fused_computation.13 | convolution fusion | flops 9059696640 | bytes 23822336 | tf_op jit(solution)/shard_map/kjtf,cf->kjtc/dot_general | solution.py:54
  1030.6 55.9 %all-gather.8.cloned.1.call-done = bf16[8,256,3456]{2,1,0:T(8,128)(2,1)} async-done(((bf16[1,256,3456]{2,1,0:T(8,128)(2,1)}), bf16[8,256,3456]{2,1,0:T(8,128)(2,1)}) %all-gather.8.cloned.1.call-update) | async-done | bytes 14155792 | tf_op jit(solution)/shard_map/all_gather | solution.py:39
  1086.6 17.4 %fusion.25 = f32[4,8,64,640]{3,2,0,1:T(8,128)} fusion(bf16[8,4,64,3456]{3,2,1,0:T(8,128)(2,1)} %bitcast.137, bf16[3456,640]{1,0:T(8,128)(2,1)} %param.8), kind=kOutput, calls=%fused_computation.27 | convolution fusion | flops 9059696640 | bytes 23822336 | tf_op jit(solution)/shard_map/dot_general | solution.py:40
  1104.0 56.6 %all-gather.10.cloned.1.call-done = bf16[8,256,3456]{2,1,0:T(8,128)(2,1)} async-done(((bf16[1,256,3456]{2,1,0:T(8,128)(2,1)}), bf16[8,256,3456]{2,1,0:T(8,128)(2,1)}) %all-gather.10.cloned.1.call-update) | async-done | bytes 14155792 | tf_op jit(solution)/shard_map/all_gather | solution.py:50
  1160.5 18.2 %add_bitcast_fusion = f32[4,8,64,640]{3,2,0,1:T(8,128)} fusion(f32[8,4,64,640]{3,2,1,0:T(8,128)} %fusion.15, bf16[8,4,64,3456]{3,2,1,0:T(8,128)(2,1)} %bitcast.141, bf16[640,3456]{1,0:T(8,128)(2,1)} %param.6), kind=kOutput, calls=%fused_computation.12 | convolution fusion | flops 9061007360 | bytes 29065216 | tf_op jit(solution)/shard_map/kjtf,cf->kjtc/dot_general | solution.py:54
  1178.8 0.6 copy-done.4
  1179.4 0.7 dynamic-slice.4
  1180.0 15.8 %fusion.6 = f32[640,3456]{0,1:T(8,128)} fusion(bf16[4,8,64,640]{3,2,1,0:T(8,128)(2,1)S(1)} %bitcast.149, bf16[8,4,64,3456]{3,2,1,0:T(8,128)(2,1)} %bitcast.142), kind=kOutput, calls=%fused_computation.9 | convolution fusion | flops 9059696640 | bytes 25624576 | tf_op jit(solution)/shard_map/jktc,kjtf->cf/dot_general | solution.py:52
  1195.9 171.6 %all-reduce.12.cloned.1.call-done = (f32[4,8,64,640]{3,2,0,1:T(8,128)}, f32[4,8,64,640]{3,2,0,1:T(8,128)}) async-done(((f32[4,8,64,640]{3,2,0,1:T(8,128)}, f32[4,8,64,640]{3,2,0,1:T(8,128)}), (f32[4,8,64,640]{3,2,0,1:T(8,128)}, f32[4,8,64,640]{3,2,0,1:T(8,128)})) %all-reduce.12.cloned.1.call-update) | async-done | bytes 10485776
  1367.5 3.0 fusion.31
  1370.5 5.2 all-to-all-start.3
  1375.7 15.8 %fusion.9 = f32[640,3456]{0,1:T(8,128)} fusion(bf16[4,8,64,640]{3,2,1,0:T(8,128)(2,1)S(1)} %bitcast.150, bf16[8,4,64,3456]{3,2,1,0:T(8,128)(2,1)} %bitcast.140), kind=kOutput, calls=%fused_computation.10 | convolution fusion | flops 9059696640 | bytes 25624576 | tf_op jit(solution)/shard_map/jktc,kjtf->cf/dot_general | solution.py:53
  1391.5 3.0 fusion.33
  1394.5 5.2 all-to-all-start.1
  1399.7 16.5 %fusion.12 = f32[3456,640]{1,0:T(8,128)} fusion(bf16[4,8,64,640]{3,2,1,0:T(8,128)(2,1)} %bitcast.146, bf16[8,4,64,3456]{3,2,1,0:T(8,128)(2,1)} %bitcast.138), kind=kOutput, calls=%fused_computation.11 | convolution fusion | flops 9059696640 | bytes 25624576 | tf_op jit(solution)/shard_map/kjtf,jktc->fc/dot_general | solution.py:49
  1416.2 10.3 copy.40
  1426.6 10.3 copy.41
  1436.9 0.9 copy.59
  1437.8 0.9 copy.58
  (20 shorter events, 0.1 us)
Async XLA Ops:
  7.2 18.2 %copy-start.2 = (bf16[64,5120]{1,0:T(8,128)(2,1)S(1)}, bf16[64,5120]{1,0:T(8,128)(2,1)}, u32[]{:S(2)}) copy-start(bf16[64,5120]{1,0:T(8,128)(2,1)} %param.9) | copy-start | bytes 1966084
  7.2 51.6 %all-gather.14.cloned.1.call-start = ((), (), s32[]{:S(2)}) async-start(), calls=%async_computation.7 | async-start | bytes 3276800 | tf_op jit(solution)/shard_map/all_gather | solution.py:30
  25.3 68.1 %all-gather.16.cloned.1.call-start = ((), (), s32[]{:S(2)}) async-start(), calls=%async_computation.8 | async-start | bytes 3276800 | tf_op jit(solution)/shard_map/all_gather | solution.py:44
  40.3 38.0 %slice-start = ((s8[4423680]{0:T(1024)(128)(4,1)}), s8[229376]{0:T(1024)(128)(4,1)S(1)}, s32[]{:S(2)}) async-start(s8[4423680]{0:T(1024)(128)(4,1)} %bitcast.143), calls=%async_computation.11 | async-start | bytes 458752
  40.4 889.8 %all-reduce.10.cloned.1.call-start = ((), (), s32[]{:S(2)}) async-start(), calls=%async_computation.9 | async-start | bytes 169869312
  58.7 19.6 %slice-start.1 = ((s8[4423680]{0:T(1024)(128)(4,1)}), s8[4194304]{0:T(1024)(128)(4,1)S(1)}, s32[]{:S(2)}) async-start(s8[4423680]{0:T(1024)(128)(4,1)} %bitcast.143), calls=%async_computation.12 | async-start | bytes 8388608
  58.8 19.6 %copy-start.3 = (bf16[32,64,640]{2,1,0:T(8,128)(2,1)S(1)}, bf16[32,64,640]{2,1,0:T(8,128)(2,1)}, u32[]{:S(2)}) copy-start(bf16[32,64,640]{2,1,0:T(8,128)(2,1)} %all-gather.14.cloned.1.call-done) | copy-start | bytes 7864324
  112.8 0.7 copy-start.5
  112.8 900.4 %all-gather.12.cloned.1.call-start = ((), (), s32[]{:S(2)}) async-start(), calls=%async_computation.6 | async-start | bytes 15925248 | tf_op jit(solution)/shard_map/all_gather | solution.py:51
  941.0 145.5 %all-gather.8.cloned.1.call-start = ((), (), s32[]{:S(2)}) async-start(), calls=%async_computation.4 | async-start | bytes 15925248 | tf_op jit(solution)/shard_map/all_gather | solution.py:39
  941.7 218.9 %all-gather.10.cloned.1.call-start = ((), (), s32[]{:S(2)}) async-start(), calls=%async_computation.5 | async-start | bytes 15925248 | tf_op jit(solution)/shard_map/all_gather | solution.py:50
  942.3 425.2 %all-reduce.12.cloned.1.call-start = ((), (), s32[]{:S(2)}) async-start(), calls=%async_computation.10 | async-start | bytes 20971520
  1178.7 0.7 copy-start.4
  1180.0 187.5 %copy-start.1 = (bf16[8,64,640]{2,1,0:T(8,128)(2,1)S(1)}, bf16[8,64,640]{2,1,0:T(8,128)(2,1)}, u32[]{:S(2)}) copy-start(bf16[8,64,640]{2,1,0:T(8,128)(2,1)} %all_to_all.21) | copy-start | bytes 1966084
  1370.5 24.0 %all-to-all-start.3 = ((bf16[8,64,640]{2,1,0:T(8,128)(2,1)}), bf16[8,64,640]{2,1,0:T(8,128)(2,1)S(1)}, u32[]{:S(2)}, u32[]{:S(2)}) async-start(bf16[8,64,640]{2,1,0:T(8,128)(2,1)} %fusion.31), calls=%async_computation.3 | async-start | bytes 1310720 | tf_op jit(solution)/shard_map/all_to_all | solution.py:22
  1375.7 15.8 %copy-start = (bf16[8,64,640]{2,1,0:T(8,128)(2,1)S(1)}, bf16[8,64,640]{2,1,0:T(8,128)(2,1)}, u32[]{:S(2)}) copy-start(bf16[8,64,640]{2,1,0:T(8,128)(2,1)} %all_to_all.20) | copy-start | bytes 1966084
  1394.5 43.3 %all-to-all-start.1 = ((bf16[8,64,640]{2,1,0:T(8,128)(2,1)}), bf16[8,64,640]{2,1,0:T(8,128)(2,1)S(1)}, u32[]{:S(2)}, u32[]{:S(2)}) async-start(bf16[8,64,640]{2,1,0:T(8,128)(2,1)} %fusion.33), calls=%async_computation.1 | async-start | bytes 1310720 | tf_op jit(solution)/shard_map/all_to_all | solution.py:22
Sparse Core Ops, SparseCore 0:
  25.4 33.2 all-gather.13
  60.3 32.4 all-gather.15
  113.0 817.2 all-reduce.9
  941.2 71.9 all-gather.11
  1014.6 71.8 all-gather.7
  1088.6 71.8 all-gather.9
  1178.9 188.5 all-reduce.11
where the time goes:
time: 1460 us; the launch traced here: 1450 us
  waiting for transfers between devices  1190 us (82%)
  matrix products  155 us (11%)
  local copies, waits for them, and re-layouts  33.3 us (2%)
  blocking collectives  31.5 us (2%)
  between operations  14.7 us (1%)
    unnamed x9, waiting for transfers between devices  989 us
    all_gather x1, waiting for transfers between devices, f(): lax.all_gather(db, 'dp', axis=0, tiled=False).reshape(nx, ny, td, fc)  70.8 us
    all_gather x1, waiting for transfers between devices, f(): lax.all_gather(da, 'dp', axis=0, tiled=False).reshape(nx, ny, td, fc)  56.6 us
    all_gather x1, waiting for transfers between devices, f(): h_all = lax.all_gather(h, 'dp', axis=0, tiled=False).reshape(nx, ny, td, fc)  55.9 us
    all_to_all x2, blocking collectives, to_cols(): return lax.all_to_all(t, 'dp', 0, 0, tiled=True)  31.5 us
    unnamed x24, local copies, waits for them, and re-layouts  31.3 us
  transfers between devices with their start and end apart: 9, of which 6 were waited for; matrix products, arithmetic and copies ran while one was open for 10% of the time, Pallas kernels for 0%

commit v1 on v0

v1 whole, which is shorter than its diff:
```python
import functools

import jax
import jax.numpy as jnp
from jax import lax
from jax.experimental import pallas as pl
from jax.experimental.pallas import tpu as pltpu
from jax.sharding import PartitionSpec as P

F32, BF16 = jnp.float32, jnp.bfloat16
LANES, ROWS = 128, 16
VMEM_LIMIT = 66_000_000


class Sizes:
    def __init__(self, axes, nx, ny, x, wg):
        self.axes = axes
        self.nc, self.ny = nx // 2, ny
        self.td, self.d = x.shape
        self.dp, self.fc = wg.shape
        self.dc = 2 * self.dp
        tiles = self.fc // LANES
        per = -(-tiles // self.nc)
        self.over = (self.nc * per - tiles) * LANES
        self.ft = per * LANES
        self.nf = self.nc * self.ft
        self.nb = self.nc * ny
        self.nj = self.td // ROWS
        self.mc = self.nb * ROWS

    def first(self, c):
        return c * self.ft - (c // (self.nc - 1)) * self.over


def _dot(a, b, ca, cb):
    return lax.dot_general(a, b, (((ca,), (cb,)), ((), ())), preferred_element_type=F32)


def _kernel(z, x_ref, wg_ref, wu_ref, wd_ref, dy_ref,
            y_ref, dx_ref, dwg_ref, dwu_ref, dwd_ref,
            xh, xp, wgu, wdb, wgup, wdp, ha, dda, rsb,
            xs, xr, ys, yr, ws, wr, ps, pr, es, er, ags, agr, rss, rsr, a2s, a2r, ls):
    nc, ny, nj = z.nc, z.ny, z.nj
    ft, dp, dc, nf, mc, td = z.ft, z.dp, z.dc, z.nf, z.mc, z.td
    half = td // 2
    me = lax.axis_index("dp")
    t = lax.axis_index("tp")
    part = lax.axis_index("part")
    c, k = me // 2, me % 2

    def dev(cc, tt, kk):
        ids = {"part": part, "tp": tt, "dp": 2 * cc + kk}
        return tuple(ids[a] for a in z.axes)

    def cx(i):
        return (c + i + nc) % nc

    def ty(i):
        return (t + i + ny) % ny

    right, left = dev(cx(1), t, k), dev(cx(-1), t, k)
    up, down = dev(c, ty(1), k), dev(c, ty(-1), k)
    mate = dev(c, t, 1 - k)

    def rc(src, dst, s, r, to):
        return pltpu.make_async_remote_copy(
            src_ref=src, dst_ref=dst, send_sem=s, recv_sem=r, device_id=to,
            device_id_type=pl.DeviceIdType.MESH)

    def lane(i, n):
        return pl.ds(pl.multiple_of(i, LANES), n)

    def row(i, n):
        return pl.ds(pl.multiple_of(i, ROWS), n)

    barrier = pltpu.get_barrier_semaphore()
    peers = [dev(cx(i), t, k) for i in range(1, nc)] + [dev(c, ty(i), k) for i in range(1, ny)] + [mate]
    for peer in peers:
        pl.semaphore_signal(barrier, inc=1, device_id=peer, device_id_type=pl.DeviceIdType.MESH)
    pl.semaphore_wait(barrier, len(peers))

    src = (x_ref, dy_ref)
    TOP, BOT = pl.ds(0, half), pl.ds(half, half)

    def blk(tt, cc):
        return tt * nc + cc

    own = blk(t, c)

    def x_send(a):
        for i, to in ((0, right), (1, left)):
            rc(src[a], xh.at[a, own], xs.at[a, i], xr.at[a, i], to).start()

    def x_pass(a):
        for i, cc, rows, to in ((0, cx(-1), TOP, right), (1, cx(1), BOT, left)):
            b = xh.at[a, blk(t, cc)]
            rc(b, b, xs.at[a, i], xr.at[a, i], to).wait_recv()
            v = xh.at[a, blk(t, cc), rows]
            rc(v, v, xs.at[a, 2 + i], xr.at[a, 2 + i], to).start()

    def x_last(a):
        for i, rows in ((2, TOP), (3, BOT)):
            v = xh.at[a, blk(t, cx(2)), rows]
            rc(v, v, xs.at[a, i], xr.at[a, i], right).wait_recv()

    OFFS = (0, -1, 1, 2)

    def y_send(a, o):
        d = xh.at[a, blk(t, cx(OFFS[o]))]
        s = src[a] if o == 0 else d
        for i, to in ((0, up), (1, down)):
            rc(s, d, ys.at[a, o, i], yr.at[a, o, i], to).start()

    def y_pass(a, o):
        for i, tt, rows, to in ((0, ty(-1), TOP, up), (1, ty(1), BOT, down)):
            b = xh.at[a, blk(tt, cx(OFFS[o]))]
            rc(b, b, ys.at[a, o, i], yr.at[a, o, i], to).wait_recv()
            v = xh.at[a, blk(tt, cx(OFFS[o])), rows]
            rc(v, v, ys.at[a, o, 2 + i], yr.at[a, o, 2 + i], to).start()

    def y_last(a, o):
        for i, rows in ((2, TOP), (3, BOT)):
            v = xh.at[a, blk(ty(2), cx(OFFS[o])), rows]
            rc(v, v, ys.at[a, o, i], yr.at[a, o, i], up).wait_recv()

    def e_copy(a):
        return rc(xh.at[a, :, :, lane((2 * c + 1 - k) * dp, dp)], xp.at[a], es.at[a], er.at[a], mate)

    def w_in(w, cc):
        if w == 2:
            return wd_ref.at[row(z.first(cc), ft), :]
        return (wg_ref, wu_ref)[w].at[:, lane(z.first(cc), ft)]

    def w_slot(w, cc, kk):
        return wdb.at[cc, kk] if w == 2 else wgu.at[w, cc, kk]

    def w_send(w):
        for i in (1, 3, 2):
            rc(w_in(w, cx(i)), w_slot(w, c, k), ws.at[w, i - 1], wr.at[w, i - 1], dev(cx(i), t, k)).start()

    def w_mate(w):
        rc(w_in(w, c), w_slot(w, c, k), ps.at[w, 0], pr.at[w, 0], mate).start()

    def w_pass(w, i):
        v = w_slot(w, cx(-i), k)
        rc(v, v, ws.at[w, i - 1], wr.at[w, i - 1], mate).wait_recv()
        rc(v, v, ps.at[w, i], pr.at[w, i], mate).start()

    def w_got(w, i):
        v = w_slot(w, cx(-i), 1 - k)
        rc(v, v, ps.at[w, i], pr.at[w, i], mate).wait_recv()

    def p_copy(w):
        s = (wg_ref, wu_ref, wd_ref)[w]
        d = wdp if w == 2 else wgup.at[w]
        return rc(s, d, es.at[2 + w], er.at[2 + w], mate)

    def local(i):
        if i < 2:
            return pltpu.make_async_copy(src[i], xh.at[i, own], ls.at[i])
        return pltpu.make_async_copy(w_in(i - 2, c), w_slot(i - 2, c, k), ls.at[i])

    def g_buf(q, j, kk, cc):
        return (dda if q else ha).at[j, kk, cc]

    def g_half(q, j, kk, cc, i):
        return dda.at[j, kk, cc, i] if q else ha.at[j, kk, cc, pl.ds(i * (mc // 2), mc // 2)]

    def g_send(q, j):
        s = nj * q + j
        v = g_buf(q, j, k, c)
        for i, to in ((0, right), (1, left), (4, mate)):
            rc(v, v, ags.at[s, i], agr.at[s, i], to).start()

    def g_pass(q, j):
        s = nj * q + j
        for i, cc, to in ((0, cx(-1), right), (1, cx(1), left)):
            v = g_buf(q, j, k, cc)
            rc(v, v, ags.at[s, i], agr.at[s, i], to).wait_recv()
            u = g_half(q, j, k, cc, i)
            rc(u, u, ags.at[s, 2 + i], agr.at[s, 2 + i], to).start()
            rc(v, v, ags.at[s, 5 + i], agr.at[s, 5 + i], mate).start()

    def g_last(q, j):
        s = nj * q + j
        for i in (0, 1):
            u = g_half(q, j, k, cx(2), i)
            rc(u, u, ags.at[s, 2 + i], agr.at[s, 2 + i], right).wait_recv()
            rc(u, u, ags.at[s, 7 + i], agr.at[s, 7 + i], mate).start()

    def g_mate(q, j):
        s = nj * q + j
        for i, cc in ((4, c), (5, cx(-1)), (6, cx(1))):
            v = g_buf(q, j, 1 - k, cc)
            rc(v, v, ags.at[s, i], agr.at[s, i], mate).wait_recv()
        for i in (0, 1):
            u = g_half(q, j, 1 - k, cx(2), i)
            rc(u, u, ags.at[s, 7 + i], agr.at[s, 7 + i], mate).wait_recv()

    def g_sent(q, j):
        s = nj * q + j
        for i in (0, 1, 4, 5, 6):
            v = g_buf(q, j, k, c)
            rc(v, v, ags.at[s, i], agr.at[s, i], mate).wait_send()
        for i in (2, 3, 7, 8):
            u = g_half(q, j, k, c, 0)
            rc(u, u, ags.at[s, i], agr.at[s, i], mate).wait_send()

    x_send(0)
    y_send(0, 0)
    x_send(1)
    for i in range(5):
        local(i).start()
    for w in range(3):
        w_mate(w)
    x_pass(0)
    y_send(0, 1)
    y_send(0, 2)
    x_pass(1)
    for w in range(3):
        p_copy(w).start()
    x_last(0)
    y_send(0, 3)
    for w in range(3):
        w_send(w)
    x_last(1)
    for o in range(4):
        y_send(1, o)
    for o in range(4):
        y_pass(0, o)
    for i in range(5):
        local(i).wait()
    for o in range(4):
        y_last(0, o)
    e_copy(0).start()

    def phase1(acc, xv, wv, wdv, hv, dv, sem):
        def x_load(a, i, slot):
            cols = lane(cx(OFFS[i]) * dc, dc)
            return [pltpu.make_async_copy(xh.at[a, :, pl.ds(j * ROWS, ROWS), cols], xv.at[slot, j], sem.at[slot, j])
                    for j in range(nj)]

        def w_load(w, i, slot):
            cc = cx(OFFS[i])
            if w == 2:
                return [pltpu.make_async_copy(wdb.at[cc, kk], wdv.at[slot, :, pl.ds(kk * dp, dp)], sem.at[slot, nj + kk])
                        for kk in range(2)]
            return [pltpu.make_async_copy(wgu.at[w, cc], wv.at[slot], sem.at[slot, nj])]

        def matmul(w, first, slot):
            @pl.loop(0, nj)
            def _(j):
                rows = row(j * mc, mc)
                lhs = xv[slot, j].reshape(mc, dc)
                if w == 2:
                    r = _dot(lhs, wdv[slot], 1, 1)
                else:
                    r = _dot(lhs, wv[slot].reshape(dc, ft), 1, 0)
                acc[w, rows, :] = r if first else acc[w, rows, :] + r

        def product(w):
            loads = {}
            for i in range(4):
                loads[i] = x_load(w // 2, i, i % 2)
            for cp in loads[0]:
                cp.start()
            for i, off in enumerate(OFFS):
                if off == 0:
                    w_got(w, 0)
                else:
                    w_got(w, -off if off < 0 else nc - off)
                wl = w_load(w, i, i % 2)
                for cp in wl:
                    cp.start()
                if i < 3:
                    for cp in loads[i + 1]:
                        cp.start()
                for cp in loads[i] + wl:
                    cp.wait()
                matmul(w, i == 0, i % 2)

        keep = lax.broadcasted_iota(jnp.int32, (ROWS, ft), 1) >= (c // (nc - 1)) * z.over

        for i in (1, 3, 2):
            w_pass(0, i)
        product(0)
        for o in range(4):
            y_pass(1, o)
        for i in (1, 3, 2):
            w_pass(1, i)
        product(1)

        @pl.loop(0, nj)
        def _(j):
            @pl.loop(0, z.nb)
            def _(b):
                rows = row(j * mc + b * ROWS, ROWS)
                aa = acc[0, rows, :]
                h = aa * jax.nn.sigmoid(aa) * acc[1, rows, :]
                hv[j, row(b * ROWS, ROWS), :] = jnp.where(keep, h, 0.0).astype(BF16)

            pltpu.make_async_copy(hv.at[j], ha.at[j, k, c], sem.at[0, 0]).start()
            pltpu.make_async_copy(hv.at[j], ha.at[j, k, c], sem.at[0, 0]).wait()

        g_send(0, 0)
        g_send(0, 1)
        for o in range(4):
            y_last(1, o)
        e_copy(1).start()
        for i in (1, 3, 2):
            w_pass(2, i)
        product(2)

        @pl.loop(0, nj)
        def _(j):
            @pl.loop(0, z.nb)
            def _(b):
                rows = row(j * mc + b * ROWS, ROWS)
                aa, gg = acc[0, rows, :], acc[2, rows, :]
                sig = jax.nn.sigmoid(aa)
                da = gg * acc[1, rows, :] * sig * (1.0 + aa * (1.0 - sig))
                db = gg * (aa * sig)
                dv[j, 0, row(b * ROWS, ROWS), :] = jnp.where(keep, da, 0.0).astype(BF16)
                dv[j, 1, row(b * ROWS, ROWS), :] = jnp.where(keep, db, 0.0).astype(BF16)

            pltpu.make_async_copy(dv.at[j], dda.at[j, k, c], sem.at[0, 0]).start()
            pltpu.make_async_copy(dv.at[j], dda.at[j, k, c], sem.at[0, 0]).wait()

    pl.run_scoped(
        phase1,
        pltpu.VMEM((3, nj * mc, ft), F32),
        pltpu.VMEM((2, nj, z.nb, ROWS, dc), BF16),
        pltpu.VMEM((2, 2, dp, ft), BF16),
        pltpu.VMEM((2, ft, dc), BF16),
        pltpu.VMEM((nj, mc, ft), BF16),
        pltpu.VMEM((nj, 2, mc, ft), BF16),
        pltpu.SemaphoreType.DMA((2, nj + 2)),
    )

    def cols_of(i):
        return pl.ds(z.first(i), ft), pl.ds(i * ft, ft)

    def tok_load(a, j, tv, sem):
        rows = pl.ds(pl.multiple_of(j * ROWS, ROWS), ROWS)
        return [pltpu.make_async_copy(xh.at[a, :, rows, lane(me * dp, dp)], tv.at[0], sem.at[0]),
                pltpu.make_async_copy(xp.at[a, :, rows, :], tv.at[1], sem.at[1])]

    rpt = nc * ROWS

    def rs_copy(q, j, i, pv, slot):
        s = nj * q + j
        return rc(pv.at[slot, row(ty(i) * rpt, rpt), :], rsb.at[s, i - 1], rss.at[s, i - 1], rsr.at[s, i - 1],
                  dev(c, ty(i), k))

    def out_copy(q, j, i, ov):
        s = nj * q + j
        dst = (dx_ref if q else y_ref).at[row(j * ROWS, ROWS), lane(c * dc, dc)]
        return rc(ov.at[cx(i)], dst, a2s.at[s, i - 1], a2r.at[s, i - 1], dev(cx(i), t, k))

    def out_local(q, j, ov, sem):
        dst = (dx_ref if q else y_ref).at[row(j * ROWS, ROWS), lane(c * dc, dc)]
        return pltpu.make_async_copy(ov.at[c], dst, sem)

    def finish(q, j, slot, pv, rv, xv, ov, sem):
        s = nj * q + j
        for i in range(1, ny):
            rs_copy(q, j, i, pv, slot).wait_recv()
        ld = [pltpu.make_async_copy(rsb.at[s], rv, sem.at[0]),
              pltpu.make_async_copy(xh.at[q, pl.ds(t * nc, nc), row(j * ROWS, ROWS), lane(c * dc, dc)],
                                    xv, sem.at[1])]
        for cp in ld:
            cp.start()

        @pl.when(j > 0)
        def _():
            for i in range(1, nc):
                out_copy(q, j - 1, i, ov).wait_send()
            out_local(q, j - 1, ov, sem.at[2]).wait()
        for cp in ld:
            cp.wait()
        for cc in range(nc):
            mine = pv[slot, row(t * rpt + cc * ROWS, ROWS), :]
            tot = mine
            for i in range(ny - 1):
                tot = tot + rv[i, pl.ds(cc * ROWS, ROWS), :]
            ov[cc] = (xv[cc].astype(F32) + tot).astype(BF16)
        for i in range(1, nc):
            out_copy(q, j, i, ov).start()
        out_local(q, j, ov, sem.at[2]).start()

    def drain(q, j, ov, sem):
        for i in range(1, nc):
            out_copy(q, j, i, ov).wait_send()
        out_local(q, j, ov, sem.at[2]).wait()

    STEP = 512

    def phase2h(acc, wv, hv, tv, pv, rv, xv, ov, sem, fsem):
        loads = []
        for i in range(nc):
            a, b = cols_of(i)
            loads.append(pltpu.make_async_copy(wd_ref.at[a, :], wv.at[b, lane(k * dp, dp)], sem.at[i]))
            loads.append(pltpu.make_async_copy(wdp.at[a, :], wv.at[b, lane((1 - k) * dp, dp)], sem.at[nc + i]))
        p_copy(2).wait_recv()
        for cp in loads:
            cp.start()
        for cp in loads:
            cp.wait()

        @pl.loop(0, nj)
        def _(j):
            slot = j % 2

            @pl.when(j < nj - 1)
            def _():
                g_pass(0, j + 1)

            @pl.when(j == nj - 1)
            def _():
                g_pass(1, 0)

            @pl.when(j < nj - 2)
            def _():
                g_send(0, j + 2)

            @pl.when(j >= nj - 2)
            def _():
                g_send(1, j - (nj - 2))
            g_last(0, j)
            mine = [pltpu.make_async_copy(ha.at[j, k, i], hv.at[pl.ds(0, mc), pl.ds(i * ft, ft)], sem.at[i])
                    for i in range(nc)]
            for cp in mine:
                cp.start()
            tl = tok_load(1, j, tv, fsem.at[1])
            for cp in tl:
                cp.start()
            for cp in mine:
                cp.wait()

            @pl.when(j >= 2)
            def _():
                for i in range(1, ny):
                    rs_copy(0, j - 2, i, pv, slot).wait_send()
            pv[slot] = _dot(hv[pl.ds(0, mc), :], wv[...], 1, 0)
            for i in range(1, ny):
                rs_copy(0, j, i, pv, slot).start()
            g_mate(0, j)
            other = [pltpu.make_async_copy(ha.at[j, 1 - k, i], hv.at[pl.ds(mc, mc), pl.ds(i * ft, ft)], sem.at[i])
                     for i in range(nc)]
            for cp in other:
                cp.start()
            for cp in tl + other:
                cp.wait()

            @pl.loop(0, nf // STEP)
            def _(n):
                r = _dot(hv[:, lane(n * STEP, STEP)], tv[...].reshape(2 * mc, dp), 0, 0)
                rows = row(n * STEP, STEP)

                @pl.when(j == 0)
                def _():
                    acc[rows, :] = r

                @pl.when(j > 0)
                def _():
                    acc[rows, :] += r

            @pl.when(j > 0)
            def _():
                finish(0, j - 1, 1 - slot, pv, rv, xv, ov, fsem.at[0])

        last = (nc - 1) * ft
        outs = [pltpu.make_async_copy(acc.at[pl.ds(0, last), :], dwd_ref.at[pl.ds(0, last), :], sem.at[0]),
                pltpu.make_async_copy(acc.at[pl.ds(last + z.over, ft - z.over), :],
                                      dwd_ref.at[pl.ds(last, ft - z.over), :], sem.at[1])]
        for cp in outs:
            cp.start()
        finish(0, nj - 1, (nj - 1) % 2, pv, rv, xv, ov, fsem.at[0])
        for j in (nj - 2, nj - 1):
            for i in range(1, ny):
                rs_copy(0, j, i, pv, j % 2).wait_send()
        drain(0, nj - 1, ov, fsem.at[0])
        for cp in outs:
            cp.wait()

    g_pass(0, 0)
    e_copy(1).wait_recv()
    e_copy(0).wait_recv()
    small = (
        pltpu.VMEM((2, z.nb, ROWS, dp), BF16),
        pltpu.VMEM((2, mc, dc), F32),
        pltpu.VMEM((ny - 1, rpt, dc), F32),
        pltpu.VMEM((nc, ROWS, dc), BF16),
        pltpu.VMEM((nc, ROWS, dc), BF16),
        pltpu.SemaphoreType.DMA((4 * nc,)),
        pltpu.SemaphoreType.DMA((2, 3)),
    )
    pl.run_scoped(
        phase2h,
        pltpu.VMEM((nf, dp), F32),
        pltpu.VMEM((nf, dc), BF16),
        pltpu.VMEM((2 * mc, nf), BF16),
        *small,
    )

    def phase2d(acc, wv, dv, tv, pv, rv, xv, ov, sem, fsem):
        loads = []
        for w, r in ((0, wg_ref), (1, wu_ref)):
            p_copy(w).wait_recv()
            for i in range(nc):
                a, b = cols_of(i)
                loads.append(pltpu.make_async_copy(r.at[:, a], wv.at[w, row(k * dp, dp), b], sem.at[(2 * w) * nc + i]))
                loads.append(pltpu.make_async_copy(wgup.at[w, :, a], wv.at[w, row((1 - k) * dp, dp), b], sem.at[(2 * w + 1) * nc + i]))
        for cp in loads:
            cp.start()
        for cp in loads:
            cp.wait()

        @pl.loop(0, nj)
        def _(j):
            slot = j % 2

            @pl.when(j < nj - 1)
            def _():
                g_pass(1, j + 1)

            @pl.when(j < nj - 2)
            def _():
                g_send(1, j + 2)
            g_last(1, j)
            mine = [pltpu.make_async_copy(dda.at[j, k, i, q], dv.at[q, pl.ds(0, mc), pl.ds(i * ft, ft)], sem.at[2 * i + q])
                    for i in range(nc) for q in range(2)]
            tl = tok_load(0, j, tv, fsem.at[1])
            for cp in tl:
                cp.start()
            for cp in mine:
                cp.start()
            for cp in mine:
                cp.wait()

            @pl.when(j >= 2)
            def _():
                for i in range(1, ny):
                    rs_copy(1, j - 2, i, pv, slot).wait_send()
            pv[slot] = _dot(dv[0, pl.ds(0, mc), :], wv[0], 1, 1)
            pv[slot] += _dot(dv[1, pl.ds(0, mc), :], wv[1], 1, 1)
            for i in range(1, ny):
                rs_copy(1, j, i, pv, slot).start()
            g_mate(1, j)
            other = [pltpu.make_async_copy(dda.at[j, 1 - k, i, q], dv.at[q, pl.ds(mc, mc), pl.ds(i * ft, ft)], sem.at[2 * i + q])
                     for i in range(nc) for q in range(2)]
            for cp in other:
                cp.start()
            for cp in tl + other:
                cp.wait()

            @pl.loop(0, nf // STEP)
            def _(n):
                cols = lane(n * STEP, STEP)
                for q in range(2):
                    r = _dot(tv[...].reshape(2 * mc, dp), dv[q, :, cols], 0, 0)

                    @pl.when(j == 0)
                    def _():
                        acc[q, :, cols] = r

                    @pl.when(j > 0)
                    def _():
                        acc[q, :, cols] += r

            @pl.when(j > 0)
            def _():
                finish(1, j - 1, 1 - slot, pv, rv, xv, ov, fsem.at[0])

        last = (nc - 1) * ft
        outs = []
        for q, r in ((0, dwg_ref), (1, dwu_ref)):
            outs += [pltpu.make_async_copy(acc.at[q, :, pl.ds(0, last)], r.at[:, pl.ds(0, last)], sem.at[2 * q]),
                     pltpu.make_async_copy(acc.at[q, :, pl.ds(last + z.over, ft - z.over)],
                                           r.at[:, pl.ds(last, ft - z.over)], sem.at[2 * q + 1])]
        for cp in outs:
            cp.start()
        finish(1, nj - 1, (nj - 1) % 2, pv, rv, xv, ov, fsem.at[0])
        for j in (nj - 2, nj - 1):
            for i in range(1, ny):
                rs_copy(1, j, i, pv, j % 2).wait_send()
        for j in range(nj):
            for q in range(2):
                for i in range(1, nc):
                    out_copy(q, j, i, ov).wait_recv()
        drain(1, nj - 1, ov, fsem.at[0])
        for cp in outs:
            cp.wait()

    pl.run_scoped(
        phase2d,
        pltpu.VMEM((2, dp, nf), F32),
        pltpu.VMEM((2, dc, nf), BF16),
        pltpu.VMEM((2, 2 * mc, nf), BF16),
        *small,
    )

    for a in range(2):
        for i in range(2):
            rc(src[a], src[a], xs.at[a, i], xr.at[a, i], right).wait_send()
            v = xh.at[a, own, TOP]
            rc(v, v, xs.at[a, 2 + i], xr.at[a, 2 + i], right).wait_send()
        for o in range(4):
            for i in range(2):
                rc(src[a], src[a], ys.at[a, o, i], yr.at[a, o, i], up).wait_send()
                v = xh.at[a, own, TOP]
                rc(v, v, ys.at[a, o, 2 + i], yr.at[a, o, 2 + i], up).wait_send()
        e_copy(a).wait_send()
    for w in range(3):
        for i in range(4):
            v = w_slot(w, c, k)
            if i:
                rc(v, v, ws.at[w, i - 1], wr.at[w, i - 1], right).wait_send()
            rc(v, v, ps.at[w, i], pr.at[w, i], mate).wait_send()
        p_copy(w).wait_send()
    for q in range(2):
        for j in range(nj):
            g_sent(q, j)


def solution(mesh):
    nx, ny = mesh.shape["dp"], mesh.shape["tp"]
    axes = mesh.axis_names
    row_spec = P(("part", "dp", "tp"), None)
    win_spec = P(("part", "dp"), "tp")
    wout_spec = P(("part", "tp"), "dp")

    def f(x, wg, wu, wd, dy):
        z = Sizes(axes, nx, ny, x, wg)
        steps = 2 * z.nj
        hbm = pl.BlockSpec(memory_space=pltpu.HBM)
        s = jax.ShapeDtypeStruct
        outs = [
            s(x.shape, BF16), s(x.shape, BF16), s(wg.shape, F32), s(wg.shape, F32), s(wd.shape, F32),
            s((2, z.nb, z.td, z.d), BF16),
            s((2, z.nb, z.td, z.dp), BF16),
            s((2, z.nc, 2, z.dp, z.ft), BF16),
            s((z.nc, 2, z.ft, z.dp), BF16),
            s((2, z.dp, z.fc), BF16),
            s((z.fc, z.dp), BF16),
            s((z.nj, 2, z.nc, z.mc, z.ft), BF16),
            s((z.nj, 2, z.nc, 2, z.mc, z.ft), BF16),
            s((steps, ny - 1, z.nc * ROWS, z.dc), F32),
        ]
        sem = pltpu.SemaphoreType.DMA
        scratch = []
        for shape in ((2, 4), (2, 4, 4), (3, 3), (3, 4), (5,), (steps, 9), (steps, ny - 1), (steps, z.nc - 1)):
            scratch += [sem(shape), sem(shape)]
        scratch.append(sem((5,)))
        r = pl.pallas_call(
            functools.partial(_kernel, z),
            out_shape=outs,
            in_specs=[hbm] * 5,
            out_specs=[hbm] * len(outs),
            scratch_shapes=scratch,
            name="mlp",
            compiler_params=pltpu.CompilerParams(
                collective_id=0, has_side_effects=True, vmem_limit_bytes=VMEM_LIMIT),
        )(x, wg, wu, wd, dy)
        return tuple(r[:5])

    return jax.shard_map(f, mesh=mesh, in_specs=(row_spec, win_spec, win_spec, wout_spec, row_spec),
                         out_specs=(row_spec, row_spec, win_spec, win_spec, wout_spec), check_vma=False)
```

time: 1460 us -> 470 us (0.32)
  waiting for transfers between devices: 1190 us -> 0 us
  Pallas kernels: 0 us -> 445 us
  matrix products: 155 us -> 0 us
  blocking collectives: 31.5 us -> 0 us
    unnamed x9 -> x0, waiting for transfers between devices: 989 us -> none
    pallas_call x0 -> x1, Pallas kernels: none -> 445 us  [f(): pl.pallas_call(functools.partial(_kernel, z), out_shape=outs, in_specs=[h...]
    all_gather x5 -> x0, waiting for transfers between devices: 202 us -> none  [the longest x1 70.8 us: f(): lax.all_gather(db, 'dp', axis=0, tiled=False).reshape(nx, ny, td, fc)]
    dot_general x9 -> x0, matrix products: 155 us -> none  [the longest x1 19.6 us: f(): b_p = jnp.dot(xs2, wu, preferred_element_type=f32).reshape(ny, nx, td, fc)]
    all_to_all x2 -> x0, blocking collectives: 31.5 us -> none  [to_cols(): return lax.all_to_all(t, 'dp', 0, 0, tiled=True)]
    unnamed x24 -> x13, local copies, waits for them, and re-layouts: 31.3 us -> 22.4 us
  transfers between devices with their start and end apart: 9 -> 0, of which waited for: 6 -> 0; matrix products, arithmetic and copies ran while one was open for 10% -> 0% of each run, Pallas kernels for 0% -> 0%
where the time goes in v1:
time: 470 us; the launch traced here: 468 us
  Pallas kernels  445 us (95%)
  local copies, waits for them, and re-layouts  22.4 us (5%)
    pallas_call x1, Pallas kernels, f(): pl.pallas_call(functools.partial(_kernel, z), out_shape=outs, in_specs=[h...  445 us
    unnamed x13, local copies, waits for them, and re-layouts  22.4 us

profile of v1, /device:TPU:97, one launch (start us, length us, event | category | flops | bytes accessed | tf_op | source)
XLA Modules:
  0.0 467.6 jit_solution(2946664678287691338)
XLA Ops:
  0.6 444.6 %mlp.1 = (bf16[64,5120]{1,0:T(8,128)(2,1)}, bf16[64,5120]{1,0:T(8,128)(2,1)}, f32[640,3456]{1,0:T(8,128)}, f32[640,3456]{1,0:T(8,128)}, f32[3456,640]{1,0:T(8,12...) custom-call(bf16[64,5120]{1,0:T(8,128)(2,1)} %x_ref.1, ...), custom_call_target="tpu_custom_call" | custom-call | tf_op jit(solution)/shard_map/mlp/pallas_call | solution.py:655
  445.2 2.0 copy.15
  447.2 2.0 copy.16
  449.1 0.0 copy-start
  449.1 0.0 slice-start
  449.1 0.0 slice-start.1
  449.1 8.7 %copy.17 = f32[640,3456]{1,0:T(8,128)} copy(f32[640,3456]{1,0:T(8,128)} %get-tuple-element.22) | data formatting | bytes 17694720
  457.8 0.0 copy-done
  457.9 0.0 slice-start.2
  457.9 4.5 copy.18
  462.3 0.0 slice-done
  462.3 1.6 slice-done.1
  463.9 0.1 slice-done.2
  464.1 3.5 copy.19
  (1 shorter events, 0.0 us)
Async XLA Ops:
  449.1 8.7 %copy-start = (f32[640,3456]{1,0:T(8,128)S(1)}, f32[640,3456]{1,0:T(8,128)}, u32[]{:S(2)}) copy-start(f32[640,3456]{1,0:T(8,128)} %get-tuple-element.23) | copy-start | bytes 26542084
  449.1 13.2 %slice-start = ((s8[8847360]{0:T(1024)(128)(4,1)}), s8[4194304]{0:T(1024)(128)(4,1)S(1)}, s32[]{:S(2)}) async-start(s8[8847360]{0:T(1024)(128)(4,1)} %bitcast), calls=%async_computation | async-start | bytes 8388608
  449.1 14.8 %slice-start.1 = ((s8[8847360]{0:T(1024)(128)(4,1)}), s8[4194304]{0:T(1024)(128)(4,1)S(1)}, s32[]{:S(2)}) async-start(s8[8847360]{0:T(1024)(128)(4,1)} %bitcast), calls=%async_computation.1 | async-start | bytes 8388608
  457.9 6.2 %slice-start.2 = ((s8[8847360]{0:T(1024)(128)(4,1)}), s8[458752]{0:T(1024)(128)(4,1)S(1)}, s32[]{:S(2)}) async-start(s8[8847360]{0:T(1024)(128)(4,1)} %bitcast), calls=%async_computation.2 | async-start | bytes 917504

commit v2 on v0

v2 whole, which is shorter than its diff:
```python
import functools

import jax
import jax.numpy as jnp
from jax import lax
from jax.experimental import pallas as pl
from jax.experimental.pallas import tpu as pltpu
from jax.sharding import PartitionSpec as P

F32, BF16 = jnp.float32, jnp.bfloat16
LANES, ROWS = 128, 16
VMEM_LIMIT = 48_000_000
X, DY = PAIR = range(2)
GATE, UP, DOWN = WEIGHTS = range(3)
H, D = range(2)
OWN, RIGHT, LEFT, FAR = CHIPS = range(4)
STEPS = (0, 1, -1, 2)


class Sizes:
    def __init__(self, axes, nx, ny, x, wg):
        self.axes = axes
        self.nc, self.ny = nx // 2, ny
        self.td, self.d = x.shape
        self.dp, self.fc = wg.shape
        self.dc = 2 * self.dp
        self.ft = self.fc // self.nc
        self.nb = self.nc * ny
        self.nj = self.td // ROWS
        self.mc = self.nb * ROWS
        self.hc = self.mc // 2
        starts = [c * self.ft for c in range(self.nc)]
        self.cover = -(-max(s % LANES + self.ft for s in starts) // LANES) * LANES
        self.fp = max(s // LANES * LANES + self.cover for s in starts)
        self.fw = -(-self.fc // (4 * LANES)) * 4 * LANES


def _dot(a, b, ca, cb):
    return lax.dot_general(a, b, (((ca,), (cb,)), ((), ())), preferred_element_type=F32)


def _nn(a, b):
    return _dot(a, b, 1, 0)


def _nt(a, b):
    return _dot(a, b, 1, 1)


def _start(cps):
    for cp in cps:
        cp.start(priority=1)


def _wait(cps):
    for cp in cps:
        cp.wait()


def _lane(i, n):
    return pl.ds(pl.multiple_of(i, LANES), n)


def _row(i, n):
    return pl.ds(pl.multiple_of(i, ROWS), n)


def _head(n):
    return pl.ds(0, n)


def _half(u, n):
    return pl.ds(u * n, n)


def _clear(acc):
    n = 2 * ROWS

    @pl.loop(0, acc.shape[0] // n)
    def _(i):
        acc[_row(i * n, n), :] = jnp.zeros((n, acc.shape[1]), F32)


def _turned(v):
    return v.astype(F32).T.astype(BF16)


def _kernel(z, x_ref, wg_ref, wu_ref, wd_ref, dy_ref,
            y_ref, dx_ref, dw, dwd_ref,
            xh, xp, wt, wdt, wsl, wmt, ha, dda, rsb,
            xs, xr, ys, yr, ws, wr, ps, pr, es, er, ags, agr, rss, rsr, a2s, a2r):
    nc, ny, nj = z.nc, z.ny, z.nj
    ft, fc, dp, dc, mc, hc, td = z.ft, z.fc, z.dp, z.dc, z.mc, z.hc, z.td
    half, hn, last = td // 2, nc // 2, nj - 1
    me = lax.axis_index("dp")
    t = lax.axis_index("tp")
    part = lax.axis_index("part")
    c, k = me // 2, me % 2

    def dev(cc, tt, kk):
        ids = {"part": part, "tp": tt, "dp": 2 * cc + kk}
        return tuple(ids[a] for a in z.axes)

    def cx(i):
        return (c + i + nc) % nc

    def ty(i):
        return (t + i + ny) % ny

    def chip(o):
        return cx(o + o // 2 - 2 * (o // 3))

    right, left = dev(cx(1), t, k), dev(cx(-1), t, k)
    up, down = dev(c, ty(1), k), dev(c, ty(-1), k)
    mate = dev(c, t, 1 - k)
    kinds = (k, 1 - k)

    def rc(src, dst, s, r, to):
        return pltpu.make_async_remote_copy(
            src_ref=src, dst_ref=dst, send_sem=s, recv_sem=r, device_id=to,
            device_id_type=pl.DeviceIdType.MESH)

    def arrived(v, r, i, frm):
        rc(v, v, r.at[i], r.at[i], frm).wait_recv()

    def left_for(v, s):
        rc(v, v, s, s, mate).wait_send()

    barrier = pltpu.get_barrier_semaphore()
    peers = [dev(cx(i), t, k) for i in range(1, nc)] + [dev(c, ty(i), k) for i in range(1, ny)] + [mate]
    for peer in peers:
        pl.semaphore_signal(barrier, device_id=peer, device_id_type=pl.DeviceIdType.MESH)
    pl.semaphore_wait(barrier, len(peers))

    src = (x_ref, dy_ref)
    TOP, BOT = (_half(i, half) for i in PAIR)
    fwd = 2

    def x_send(a):
        for i, to in enumerate((right, left)):
            rc(src[a], xh.at[a, c, t], xs.at[a], xr.at[a, i], to).start()

    def x_pass(a):
        for i, (cc, rows, to) in enumerate(((cx(-1), TOP, right), (cx(1), BOT, left))):
            arrived(xh.at[a, cc, t], xr, (a, i), to)
            v = xh.at[a, cc, t, rows]
            rc(v, v, xs.at[a], xr.at[a, fwd], to).start()

    def x_last(a):
        arrived(xh.at[a, cx(2), t], xr, (a, fwd), right)

    def y_send(a, o):
        d = xh.at[a, cx(STEPS[o]), t]
        s = src[a] if o == OWN else d
        for i, to in enumerate((up, down)):
            rc(s, d, ys.at[a], yr.at[a, o, i], to).start()

    def y_pass(a, o):
        for i, (tt, rows, to) in enumerate(((ty(-1), TOP, up), (ty(1), BOT, down))):
            arrived(xh.at[a, cx(STEPS[o]), tt], yr, (a, o, i), to)
            v = xh.at[a, cx(STEPS[o]), tt, rows]
            rc(v, v, ys.at[a], yr.at[a, o, fwd], to).start()

    def y_last(a, o):
        arrived(xh.at[a, cx(STEPS[o]), ty(2)], yr, (a, o, fwd), up)

    def e_copy(a):
        return rc(xh.at[a, :, :, :, _lane((2 * c + 1 - k) * dp, dp)], xp.at[a], es.at[0], er.at[a], mate)

    def w_in(w, cc):
        return (wd_ref if w == DOWN else wt.at[w]).at[_row(cc * ft, ft), :]

    def w_send(w):
        for o in (RIGHT, LEFT, FAR):
            rc(w_in(w, cx(STEPS[o])), wsl.at[w, c, k], ws.at[w], wr.at[w, o], dev(cx(STEPS[o]), t, k)).start()

    def w_mate(w):
        rc(w_in(w, c), wsl.at[w, c, k], ps.at[w], pr.at[w, OWN], mate).start()

    def w_pass(w, o):
        v = wsl.at[w, cx(STEPS[o]), k]
        arrived(v, wr, (w, {RIGHT: LEFT, LEFT: RIGHT, FAR: FAR}[o]), mate)
        rc(v, v, ps.at[w], pr.at[w, o], mate).start()

    def w_got(w, o):
        arrived(wsl.at[w, cx(STEPS[o]), 1 - k], pr, (w, o), mate)

    def p_copy(w):
        return rc((wg_ref, wu_ref, wdt)[w], wmt.at[w], es.at[1], er.at[len(PAIR) + w], mate)

    def gs(q, j, u):
        return nj * q + j if u is None else nj + last + u

    def gv(q, j, kk, cc, u=None):
        b = (dda if q else ha).at[j, kk, cc]
        return b if u is None else b.at[:, u]

    def g_some(q, j, kk, n, u):
        b = (dda if q else ha).at[j, kk, pl.ds(0, n)]
        return b if u is None else b.at[:, :, u]

    def gp(q, j, kk, cc, i, u=None):
        b = (dda if q else ha).at[j, kk, cc, i]
        return b if u is None else b.at[u]

    HOP, PASSED, MATE_NEAR, MATE_FAR = 0, 2, 3, 4

    def g_send(q, j, u=None):
        s = gs(q, j, u)
        v = gv(q, j, k, c, u)
        for i, to in ((HOP, right), (HOP + 1, left), (MATE_NEAR, mate)):
            rc(v, v, ags.at[s, 0], agr.at[s, i], to).start()

    def g_pass(q, j, u=None):
        s = gs(q, j, u)
        for i, (cc, to) in enumerate(((cx(-1), right), (cx(1), left))):
            v = gv(q, j, k, cc, u)
            arrived(v, agr, (s, HOP + i), to)
            p = gp(q, j, k, cc, i, u)
            rc(p, p, ags.at[s, 1], agr.at[s, PASSED], to).start()
            rc(v, v, ags.at[s, 1], agr.at[s, MATE_NEAR], mate).start()

    def g_last(q, j, u=None):
        s = gs(q, j, u)
        v = gv(q, j, k, cx(2), u)
        arrived(v, agr, (s, PASSED), right)
        rc(v, v, ags.at[s, 0], agr.at[s, MATE_FAR], mate).start()

    def g_mate_near(q, j, u=None):
        arrived(g_some(q, j, 1 - k, nc - 1, u), agr, (gs(q, j, u), MATE_NEAR), mate)

    def g_mate_far(q, j, u=None):
        arrived(gv(q, j, 1 - k, cx(2), u), agr, (gs(q, j, u), MATE_FAR), mate)

    def g_sent(q, j, u=None):
        for i in PAIR:
            left_for(g_some(q, j, k, nc - i, u), ags.at[gs(q, j, u), i])

    def sent_tokens():
        for a in PAIR:
            left_for(xh.at[a, pl.ds(0, nc - 1), 0], xs.at[a])
            left_for(xh.at[a, pl.ds(0, nc - 1)], ys.at[a])
        left_for(xp, es.at[0])

    def sent_weights():
        for w in WEIGHTS:
            left_for(wsl.at[w, pl.ds(0, nc - 1), 0], ws.at[w])
            left_for(wsl.at[w, :, 0], ps.at[w])
        left_for(wmt, es.at[1])

    def phase1(acc, xb, wide, tall, xv, wv, dv, bsem, tsem, sem):
        def x_in(a):
            return pltpu.make_async_copy(src[a], xb.at[a], bsem.at[0, a])

        def x_out(a):
            return pltpu.make_async_copy(xb.at[a], xh.at[a, c, t], bsem.at[1, a])

        def place(w):
            return (tall.at[GATE], wide.at[GATE]) if w == DOWN else (wide.at[w], tall.at[w])

        def s_in(w):
            return pltpu.make_async_copy((wg_ref, wu_ref, wd_ref)[w], place(w)[0], tsem.at[0, w])

        def s_out(w):
            return pltpu.make_async_copy(place(w)[1], wdt if w == DOWN else wt.at[w], tsem.at[1, w])

        def s_own(w):
            s = place(w)[0 if w == DOWN else 1].at[_row(c * ft, ft), :]
            return pltpu.make_async_copy(s, wsl.at[w, c, k], tsem.at[2, w])

        def turned(w):
            a, b = place(w)

            @pl.loop(0, fc // LANES)
            def _(n):
                rows, cols = _row(n * LANES, LANES), _lane(n * LANES, LANES)
                if w == DOWN:
                    b[:, cols] = _turned(a[rows, :])
                else:
                    b[rows, :] = _turned(a[:, cols])
            _start([s_out(w)])
            _start([s_own(w)])

        x_send(X)
        y_send(X, OWN)
        x_send(DY)
        for w in PAIR:
            _start([s_in(w)])
        for a in PAIR:
            _start([x_in(a)])
        for w in PAIR:
            s_in(w).wait()
            turned(w)
        s_out(GATE).wait()
        s_own(GATE).wait()
        _start([s_in(DOWN)])
        for a in PAIR:
            x_in(a).wait()
            _start([x_out(a)])
        s_in(DOWN).wait()
        turned(DOWN)
        x_pass(X)
        y_send(X, RIGHT)
        y_send(X, LEFT)
        for w in WEIGHTS:
            _clear(acc.at[w])
        for w in (UP, DOWN):
            s_out(w).wait()
        for w in WEIGHTS:
            w_mate(w)
        x_pass(DY)
        x_last(X)
        y_send(X, FAR)
        w_send(GATE)
        for w in WEIGHTS:
            p_copy(w).start()
        x_last(DY)
        for w in (UP, DOWN):
            s_own(w).wait()
        for a in PAIR:
            x_out(a).wait()
        for o in CHIPS:
            y_pass(X, o)
        for o in CHIPS:
            y_send(DY, o)
        y_last(X, OWN)
        y_last(X, RIGHT)
        w_send(UP)
        w_pass(GATE, LEFT)
        w_pass(GATE, RIGHT)
        y_last(X, LEFT)
        y_last(X, FAR)

        def x_load(a, o, slot):
            cols = _lane(cx(STEPS[o]) * dc, dc)
            return [pltpu.make_async_copy(xh.at[a, :, :, pl.ds(j * ROWS, ROWS), cols], xv.at[slot, j], sem.at[slot, j])
                    for j in range(nj)]

        def w_load(w, o, slot):
            return [pltpu.make_async_copy(wsl.at[w, cx(STEPS[o]), kk], wv.at[slot, :, _half(kk, dp)], sem.at[slot, nj + kk])
                    for kk in PAIR]

        def matmul(w, slot):
            @pl.loop(0, nj)
            def _(j):
                cols = _lane(j * mc, mc)
                acc[w, :, cols] += _nt(wv[slot], xv[slot, j].reshape(mc, dc))

        n_parts = len(CHIPS)
        parts = [(w, o) for w in WEIGHTS for o in CHIPS]

        def products(before, early, after):
            def tokens(n):
                w, o = parts[n]
                _start(x_load(DY if w == DOWN else X, o, n % 2))

            def read(n):
                before(*parts[n])
                _start(w_load(*parts[n], n % 2))

            tokens(0)
            read(0)

            @pl.loop(0, len(parts))
            def _(n):
                for m, (w, o) in enumerate(parts[:-1]):
                    @pl.when(n == m)
                    def _():
                        if parts[m + 1] != (DOWN, OWN):
                            tokens(m + 1)
                        if parts[m + 1] in early:
                            read(m + 1)
                _wait(w_load(GATE, OWN, n % 2) + x_load(X, OWN, n % 2))
                matmul(n // n_parts, n % 2)
                for m, (w, o) in enumerate(parts[:-1]):
                    @pl.when(n == m)
                    def _():
                        if o == FAR:
                            after(w)
                        if parts[m + 1] == (DOWN, OWN):
                            tokens(m + 1)
                        if parts[m + 1] not in early:
                            read(m + 1)

        def h_out(j):
            return pltpu.make_async_copy(dv.at[j, 0], ha.at[j, k, c], sem.at[0, j])

        def d_out(j):
            return pltpu.make_async_copy(dv.at[j], dda.at[j, k, c], sem.at[0, j])

        step = 2 * ROWS

        def hidden():
            @pl.loop(0, nj)
            def _(j):
                @pl.loop(0, ft // step)
                def _(r):
                    rows, cols = _row(r * step, step), _lane(j * mc, mc)
                    aa = acc[GATE, rows, cols]
                    h = (aa * jax.nn.sigmoid(aa) * acc[UP, rows, cols]).astype(BF16)
                    for u in PAIR:
                        dv[j, 0, u, rows, :] = h[:, u * hc:(u + 1) * hc]
                _start([h_out(j)])
            for j in range(nj):
                h_out(j).wait()

        def grads():
            @pl.loop(0, nj)
            def _(j):
                @pl.loop(0, ft // step)
                def _(r):
                    rows, cols = _row(r * step, step), _lane(j * mc, mc)
                    aa, gg = acc[GATE, rows, cols], acc[DOWN, rows, cols]
                    sig = jax.nn.sigmoid(aa)
                    da = (gg * acc[UP, rows, cols] * sig * (1.0 + aa * (1.0 - sig))).astype(BF16)
                    db = (gg * (aa * sig)).astype(BF16)
                    for q, v in enumerate((da, db)):
                        for u in PAIR:
                            dv[j, q, u, rows, :] = v[:, u * hc:(u + 1) * hc]
                _start([d_out(j)])
            for j in range(nj):
                d_out(j).wait()

        def before(w, o):
            if (w, o) == (UP, FAR):
                y_pass(DY, LEFT)
                w_pass(UP, FAR)
                y_pass(DY, FAR)
            elif o != OWN and (w == UP or o == FAR):
                w_pass(w, o)
            w_got(w, o)

        def after(w):
            if w == GATE:
                y_pass(DY, OWN)
                y_pass(DY, RIGHT)
                w_send(DOWN)
                return
            hidden()
            g_send(H, 0)
            g_send(H, 1)
            e_copy(X).start()
            for o in CHIPS:
                y_last(DY, o)
            w_pass(DOWN, LEFT)
            w_pass(DOWN, RIGHT)

        early = [(GATE, o) for o in CHIPS] + [(UP, LEFT), (DOWN, RIGHT), (DOWN, LEFT)]
        products(before, early, after)
        e_copy(DY).start()
        grads()

    sem = pltpu.SemaphoreType.DMA
    two = len(PAIR)
    pl.run_scoped(
        phase1,
        pltpu.VMEM((len(WEIGHTS), ft, nj * mc), F32),
        pltpu.VMEM((two, td, z.d), BF16),
        pltpu.VMEM((two, dp, fc), BF16),
        pltpu.VMEM((two, fc, dp), BF16),
        pltpu.VMEM((two, nj, nc, ny, ROWS, dc), BF16),
        pltpu.VMEM((two, ft, dc), BF16),
        pltpu.VMEM((nj, two, two, ft, hc), BF16),
        sem((two, two)), sem((3, 3)), sem((two, nj + two)),
    )

    def at_of(q, j):
        return nj * q + j

    def phase2(pt, pv, rv, tv, ov, sb, ssem, fsem, lsem):
        def wide_load(dst, own, other, s):
            return [pltpu.make_async_copy(v, dst.at[_row(kk * dp, dp), _head(fc)], s.at[i])
                    for i, (v, kk) in enumerate(zip((own, other), kinds))]

        def blank(dst):
            dst[:, fc:] = jnp.zeros((dc, z.fp - fc), BF16)

        def share_load(q, j, o, u=None):
            cc, slot = chip(o), o % 2
            at = _row(cc * ft - cc * ft // LANES * LANES, ft)
            cps = []
            for i in range(1 + q):
                for v in PAIR if u is None else (u,):
                    s = dda.at[j, k, cc, i, v] if q else ha.at[j, k, cc, v]
                    cols = _half(v, hc) if u is None else _lane(v * hc, hc)
                    cps.append(pltpu.make_async_copy(s, sb.at[slot, i, at, cols], ssem.at[slot, i, v]))
            return cps

        low = min(z.cover - ft, ft)

        def share_blank(q, slot):
            for i in range(1 + q):
                for a in (0, z.cover - low):
                    sb[slot, i, pl.ds(a, low), :] = jnp.zeros((low, mc), BF16)

        def share_start(q, j, o):
            share_blank(q, o % 2)
            _start(share_load(q, j, o))

        def share(q, j, o, wc, u=None):
            _wait(share_load(q, j, o, u))
            cols = _lane(chip(o) * ft // LANES * LANES, z.cover)
            p = at_of(q, j) % 2
            at = _head(mc) if u is None else _lane(u * hc, hc)
            if q:
                @pl.loop(0, two)
                def _(i):
                    pt[p, :, at] += _nn(wc[i, :, cols], sb[o % 2, i, :, at])
            else:
                pt[p, :, at] += _nn(wc[:, cols], sb[o % 2, 0, :, at])

        def shares(q, j, wc, first, end):
            @pl.loop(first, end)
            def _(o):
                @pl.when(o + 1 < end)
                def _():
                    share_start(q, j, o + 1)
                share(q, j, o, wc)

        def front(q, j, wc):
            _clear(pt.at[at_of(q, j) % 2])
            shares(q, j, wc, OWN, FAR)

        def upright(q, j, u):
            p, s = at_of(q, j) % 2, at_of(q, j) % 3
            wide = 2 * LANES

            @pl.loop(0, dc // wide)
            def _(i):
                v = pt[p, _row(i * wide, wide), _lane(u * hc, hc)].T
                pv[s, pl.ds(u * hn, hn), :, :, _lane(i * wide, wide)] = v.reshape(hn, ny, ROWS, wide)

        def rs_copy(s, u, i):
            r = i - 1
            return rc(pv.at[s % 3, pl.ds(u * hn, hn), ty(i)], rsb.at[s, u, r], rss.at[s], rsr.at[s, u], dev(c, ty(i), k))

        def rs_send(s, u):
            for i in range(1, ny):
                rs_copy(s, u, i).start()

        def rs_free(s):
            left_for(pv.at[s % 3, :, pl.ds(0, ny - 1)], rss.at[s])

        def send_up(q, j):
            @pl.loop(0, two)
            def _(u):
                upright(q, j, u)
                rs_send(at_of(q, j), u)

        def out_rows(q, j):
            return (dx_ref if q else y_ref).at[_row(j * ROWS, ROWS), _lane(c * dc, dc)]

        def out_copy(s, dst, cc):
            return rc(ov.at[s, cc], dst, a2s.at[s], a2r.at[s], dev(cc, t, k))

        def out_local(s, dst):
            return pltpu.make_async_copy(ov.at[s, c], dst, lsem.at[s])

        def out_send(q, j):
            s, dst = at_of(q, j), out_rows(q, j)
            for cc in range(nc):
                @pl.when(cc != c)
                def _():
                    out_copy(s, dst, cc).start()
            _start([out_local(s, dst)])

        def out_done(s):
            v = ov.at[s, pl.ds(0, nc - 1)]
            left_for(v, a2s.at[s])
            arrived(v, a2r, s, mate)
            out_local(s, out_rows(H, 0)).wait()

        def finish_loads(q, j, u):
            rows = pl.ds(u * hn, hn)
            return [pltpu.make_async_copy(rsb.at[at_of(q, j), u], rv.at[u], fsem.at[0, u]),
                    pltpu.make_async_copy(xh.at[q, rows, t, _row(j * ROWS, ROWS), _lane(c * dc, dc)], tv.at[rows],
                                          fsem.at[1, u])]

        def finish_start(q, j):
            @pl.loop(0, two)
            def _(u):
                arrived(rsb.at[at_of(q, j), u], rsr, (at_of(q, j), u), mate)
                _start(finish_loads(q, j, u))

        def finish(q, j):
            s = at_of(q, j)

            @pl.loop(0, two)
            def _(u):
                _wait(finish_loads(q, j, u))
                for i in range(hn):
                    cc = u * hn + i
                    tot = pv[s % 3, cc, t]
                    for m in range(ny - 1):
                        tot = tot + rv[u, m, i]
                    ov[s, cc] = (tv[cc].astype(F32) + tot).astype(BF16)

        def tok_load(a, j, buf, s):
            rows = _row(j * ROWS, ROWS)
            return [pltpu.make_async_copy(xh.at[a, :, :, rows, _lane(me * dp, dp)], buf.at[0], s.at[0]),
                    pltpu.make_async_copy(xp.at[a, :, :, rows, :], buf.at[1], s.at[1])]

        def phase2h(acc, wc, hv, kv, psem, dsem, ksem):
            p_copy(DOWN).wait_recv()
            loads = wide_load(wc, wdt, wmt.at[DOWN], psem)
            _start(loads)
            g_pass(H, 0)
            g_send(H, 2)
            blank(wc)
            _clear(acc)
            for w in PAIR:
                p_copy(w).wait_recv()
                e_copy(w).wait_recv()
            _wait(loads)

            def h_load(j, os, hs=PAIR):
                return [pltpu.make_async_copy(ha.at[j, kinds[i], cx(STEPS[o]), u],
                                              hv.at[_row(cx(STEPS[o]) * ft, ft), pl.ds(i * mc + u * hc, hc)],
                                              dsem.at[i, o, u])
                        for i in hs for o in os for u in PAIR]

            def add_outer(first, end):
                @pl.loop(first, end)
                def _(o):
                    rows = _row(chip(o) * ft, ft)
                    acc[rows, :] += _nn(hv[rows, :], kv[...].reshape(2 * mc, dp))

            near = (OWN, RIGHT, LEFT)
            share_start(H, 0, OWN)

            @pl.loop(0, nj + 1)
            def _(j):
                here, before, two_before = j < nj, j > 0, j > 1

                @pl.when(before & here)
                def _():
                    g_pass(H, j)

                @pl.when(j == nj)
                def _():
                    g_pass(D, 0)
                    g_send(D, 2)

                @pl.when(before & (j < nj - 2))
                def _():
                    g_send(H, j + 2)

                @pl.when((j >= nj - 2) & here)
                def _():
                    g_send(D, j - (nj - 2))

                @pl.when(before)
                def _():
                    g_mate_near(H, j - 1)
                    _start(tok_load(DY, j - 1, kv, ksem))
                    _start(h_load(j - 1, near))

                @pl.when((j >= 3) & here)
                def _():
                    rs_free(j - 3)

                @pl.when(here)
                def _():
                    front(H, j, wc)

                @pl.when(before)
                def _():
                    g_last(H, j - 1)
                    share_start(H, j - 1, FAR)
                    _start(h_load(j - 1, (FAR,), (0,)))

                @pl.when(j < last)
                def _():
                    share_start(H, j + 1, OWN)

                @pl.when(j == last)
                def _():
                    share_start(D, 0, OWN)

                @pl.when(before)
                def _():
                    _wait(tok_load(DY, j - 1, kv, ksem))
                    _wait(h_load(j - 1, near))
                    add_outer(OWN, FAR)
                    shares(H, j - 1, wc, FAR, FAR + 1)
                    g_mate_far(H, j - 1)
                    _start(h_load(j - 1, (FAR,), (1,)))
                    send_up(H, j - 1)

                @pl.when(two_before)
                def _():
                    finish_start(H, j - 2)

                @pl.when(before)
                def _():
                    _wait(h_load(j - 1, (FAR,)))
                    add_outer(FAR, FAR + 1)

                @pl.when(two_before)
                def _():
                    finish(H, j - 2)

            out = pltpu.make_async_copy(acc, dwd_ref, psem.at[0])
            _start([out])
            out.wait()

        pl.run_scoped(
            phase2h,
            pltpu.VMEM((fc, dp), F32),
            pltpu.VMEM((dc, z.fp), BF16),
            pltpu.VMEM((fc, 2 * mc), BF16),
            pltpu.VMEM((two, nc, ny, ROWS, dp), BF16),
            sem((two,)), sem((two, len(CHIPS), two)), sem((two,)),
        )

        def phase2d(wc, dv, kv, kt, wsem, dsem, ksem):
            loads = [cp for w in PAIR for cp in wide_load(wc.at[w], (wg_ref, wu_ref)[w], wmt.at[w], wsem.at[w])]
            _start(loads)
            for w in PAIR:
                blank(wc.at[w])
                _clear(dw.at[w])
            dv[:, fc:] = jnp.zeros((two, z.fw - fc, 2 * mc), BF16)
            _wait(loads)

            def d_load(j, os, hs=PAIR, us=PAIR):
                return [pltpu.make_async_copy(dda.at[j, kinds[i], cx(STEPS[o]), q, u],
                                              dv.at[q, _row(cx(STEPS[o]) * ft, ft), pl.ds(i * mc + u * hc, hc)],
                                              dsem.at[i, o, q, u])
                        for i in hs for o in os for q in PAIR for u in us]

            def add_outer():
                n = z.fw // 2

                @pl.loop(0, 2 * two)
                def _(i):
                    q, cols = i // 2, _lane(i % 2 * n, n)
                    dw[q, :, cols] += _nt(kt[...], dv[q, cols, :])

            def far(j, us=(None,)):
                for u in us:
                    g_mate_far(D, j, u)
                _start(d_load(j, (FAR,), (1,)))
                _wait(tok_load(X, j, kv, ksem))

                @pl.loop(0, dp // LANES)
                def _(i):
                    v = kv[:, :, :, :, _lane(i * LANES, LANES)].reshape(2 * mc, LANES)
                    kt[_row(i * LANES, LANES), :] = _turned(v)

            def back(j):
                g_last(D, j)
                share_start(D, j, FAR)
                _start(d_load(j, (FAR,), (0,)))

            near = (OWN, RIGHT, LEFT)

            def near_start(j):
                g_mate_near(D, j)
                _start(tok_load(X, j, kv, ksem))
                _start(d_load(j, near))

            @pl.loop(0, last)
            def _(j):
                before, first = j > 0, j == 1

                @pl.when(first)
                def _():
                    sent_tokens()
                    sent_weights()

                @pl.when(before)
                def _():
                    g_pass(D, j)

                @pl.when(before & (j < last - 2))
                def _():
                    g_send(D, j + 2)

                @pl.when(j == last - 1)
                def _():
                    for u in PAIR:
                        g_send(D, last, u)
                    for i in range(nj):
                        g_sent(H, i)

                @pl.when(before)
                def _():
                    near_start(j - 1)

                rs_free(nj + j - 3)
                front(D, j, wc)

                @pl.when(before)
                def _():
                    back(j - 1)

                share_start(D, j + 1, OWN)

                @pl.when(before)
                def _():
                    shares(D, j - 1, wc, FAR, FAR + 1)
                    send_up(D, j - 1)

                @pl.when(first)
                def _():
                    finish_start(H, last)

                @pl.when(j > 1)
                def _():
                    finish_start(D, j - 2)

                @pl.when(before)
                def _():
                    far(j - 1)
                    _wait(d_load(j - 1, CHIPS))
                    add_outer()

                @pl.when(first)
                def _():
                    finish(H, last)

                @pl.when(j > 1)
                def _():
                    finish(D, j - 2)

            m = last - 1
            near_start(m)
            back(m)
            rs_free(nj + last - 3)
            _clear(pt.at[at_of(D, last) % 2])
            shares(D, m, wc, FAR, FAR + 1)
            send_up(D, m)
            finish_start(D, m - 1)
            far(m)
            shares(D, last, wc, OWN, RIGHT)
            _wait(d_load(m, CHIPS))
            add_outer()
            finish(D, m - 1)
            for i in range(m):
                g_sent(D, i)
            _start(tok_load(X, last, kv, ksem))
            for u in PAIR:
                g_pass(D, last, u)
            share_start(D, last, RIGHT)
            share_start(D, last, LEFT)
            _start(d_load(last, near, (0,)))
            share(D, last, RIGHT, wc)
            share_blank(D, FAR % 2)

            @pl.loop(0, nj)
            def _(i):
                out_send(H, i)

            @pl.loop(0, m)
            def _(i):
                out_send(D, i)
            g_last(D, last, 0)
            _start(share_load(D, last, FAR, 0))
            share(D, last, LEFT, wc)

            @pl.loop(0, two)
            def _(u):
                @pl.when(u == 1)
                def _():
                    g_last(D, last, 1)
                    _start(share_load(D, last, FAR, 1))
                share(D, last, FAR, wc, u)
                upright(D, last, u)
                rs_send(at_of(D, last), u)

                @pl.when(u == 0)
                def _():
                    finish_start(D, m)
            for u in PAIR:
                g_mate_near(D, last, u)
            _start(d_load(last, near, (1,)))
            _start(d_load(last, (FAR,), (0,)))
            finish(D, m)
            out_send(D, m)
            far(last, PAIR)
            g_sent(D, m)
            for u in PAIR:
                g_sent(D, last, u)
            _wait(d_load(last, CHIPS))
            add_outer()
            finish_start(D, last)
            finish(D, last)
            out_send(D, last)
            for i in range(3):
                rs_free(nj + last - i)

            @pl.loop(0, 2 * nj)
            def _(i):
                out_done(i)

        pl.run_scoped(
            phase2d,
            pltpu.VMEM((two, dc, z.fp), BF16),
            pltpu.VMEM((two, z.fw, 2 * mc), BF16),
            pltpu.VMEM((two, nc, ny, ROWS, dp), BF16),
            pltpu.VMEM((dp, 2 * mc), BF16),
            sem((two, two)), sem((two, len(CHIPS), two, two)), sem((two,)),
        )

    pl.run_scoped(
        phase2,
        pltpu.VMEM((two, dc, mc), F32),
        pltpu.VMEM((3, nc, ny, ROWS, dc), F32),
        pltpu.VMEM((two, ny - 1, hn, ROWS, dc), F32),
        pltpu.VMEM((nc, ROWS, dc), BF16),
        pltpu.VMEM((2 * nj, nc, ROWS, dc), BF16),
        pltpu.VMEM((two, two, z.cover, mc), BF16),
        sem((two, two, two)), sem((two, two)), sem((2 * nj,)),
    )


def _move(pieces, y, dx, dw, dwd, y_out, dx_out, dwg_out, dwu_out, dwd_out, y_buf, dx_buf, dwd_buf, sems):
    small = [(a, b, o, 1) for a, b, o in ((y, y_buf, y_out), (dx, dx_buf, dx_out))]
    moves = []
    for a, b, o, n in [(dwd, dwd_buf, dwd_out, pieces)] + small:
        rows = a.shape[0] // n
        moves += [[x.at[pl.ds(i * rows, rows)] for x in (a, b, o)] for i in range(n)]

    def copy(i, leg):
        return pltpu.make_async_copy(moves[i][leg], moves[i][leg + 1], sems.at[leg, i])

    direct = [pltpu.make_async_copy(dw.at[q, :, _head(o.shape[1])], o, sems.at[0, len(moves) + q])
              for q, o in enumerate((dwg_out, dwu_out))]
    for i in range(len(moves)):
        copy(i, 0).start()
    _start(direct)
    for i in range(len(moves)):
        copy(i, 0).wait()
        copy(i, 1).start()
    for i in range(len(moves)):
        copy(i, 1).wait()
    _wait(direct)


def _results(y, dx, dw, dwd, like, pieces):
    hbm, vmem = (pl.BlockSpec(memory_space=m) for m in (pltpu.HBM, pltpu.VMEM))
    like = jax.ShapeDtypeStruct(like.shape, F32)
    shapes = [jax.ShapeDtypeStruct(a.shape, a.dtype) for a in (y, dx)]
    return pl.pallas_call(
        functools.partial(_move, pieces),
        out_shape=shapes + [like, like, jax.ShapeDtypeStruct(dwd.shape, F32)],
        in_specs=[hbm, hbm, vmem, hbm],
        out_specs=[hbm] * 5,
        scratch_shapes=[pltpu.VMEM(a.shape, a.dtype) for a in (y, dx, dwd)]
        + [pltpu.SemaphoreType.DMA((2, pieces + 4))],
        name="results",
        compiler_params=pltpu.CompilerParams(vmem_limit_bytes=VMEM_LIMIT // 2),
    )(*(pltpu.with_memory_space_constraint(v, m)
        for v, m in ((y, pltpu.HBM), (dx, pltpu.HBM), (dw, pltpu.VMEM), (dwd, pltpu.HBM))))


def solution(mesh):
    nx, ny = mesh.shape["dp"], mesh.shape["tp"]
    axes = mesh.axis_names
    row_spec = P(("part", "dp", "tp"), None)
    win_spec = P(("part", "dp"), "tp")
    wout_spec = P(("part", "tp"), "dp")

    def f(x, wg, wu, wd, dy):
        z = Sizes(axes, nx, ny, x, wg)
        steps, two, kinds = 2 * z.nj, len(PAIR), len(WEIGHTS)
        hbm = pl.BlockSpec(memory_space=pltpu.HBM)
        vmem = pl.BlockSpec(memory_space=pltpu.VMEM)
        bf16 = functools.partial(jax.ShapeDtypeStruct, dtype=BF16)
        f32 = functools.partial(jax.ShapeDtypeStruct, dtype=F32)
        outs = [
            bf16(x.shape), bf16(x.shape), pltpu.VMEM((two, z.dp, z.fw), F32), f32(wd.shape),
            bf16((two, z.nc, ny, z.td, z.d)),
            bf16((two, z.nc, ny, z.td, z.dp)),
            bf16((two, z.fc, z.dp)),
            bf16((z.dp, z.fc)),
            bf16((kinds, z.nc, two, z.ft, z.dp)),
            bf16((kinds, z.dp, z.fc)),
            bf16((z.nj, two, z.nc, two, z.ft, z.hc)),
            bf16((z.nj, two, z.nc, two, two, z.ft, z.hc)),
            f32((steps, two, ny - 1, z.nc // 2, ROWS, z.dc)),
        ]
        specs = [hbm] * len(outs)
        specs[2] = vmem
        sem = pltpu.SemaphoreType.DMA
        chips = len(CHIPS)
        shapes = ((two,), (two, 3), (two,), (two, chips, 3), (kinds,), (kinds, chips), (kinds,), (kinds, chips),
                  (two,), (two + kinds,), (steps + 1, two), (steps + 1, 5), (steps,), (steps, two), (steps,), (steps,))
        r = pl.pallas_call(
            functools.partial(_kernel, z),
            out_shape=outs,
            in_specs=[hbm] * 5,
            out_specs=specs,
            scratch_shapes=[sem(shape) for shape in shapes],
            name="mlp",
            compiler_params=pltpu.CompilerParams(
                collective_id=0, has_side_effects=True, vmem_limit_bytes=VMEM_LIMIT),
        )(x, wg, wu, wd, dy)
        return tuple(_results(*r[:4], wg, 8))

    return jax.shard_map(f, mesh=mesh, in_specs=(row_spec, win_spec, win_spec, wout_spec, row_spec),
                         out_specs=(row_spec, row_spec, win_spec, win_spec, wout_spec), check_vma=False)
```

time: 1460 us -> 404 us (0.28)
  waiting for transfers between devices: 1190 us -> 0 us
  Pallas kernels: 0 us -> 400 us
  matrix products: 155 us -> 0 us
  local copies, waits for them, and re-layouts: 33.3 us -> 0 us
  blocking collectives: 31.5 us -> 0 us
    unnamed x9 -> x0, waiting for transfers between devices: 989 us -> none
    pallas_call x0 -> x2, Pallas kernels: none -> 400 us  [the longest x1 387 us: f(): pl.pallas_call(functools.partial(_kernel, z), out_shape=outs, in_specs=[h...]
    all_gather x5 -> x0, waiting for transfers between devices: 202 us -> none  [the longest x1 70.8 us: f(): lax.all_gather(db, 'dp', axis=0, tiled=False).reshape(nx, ny, td, fc)]
    dot_general x9 -> x0, matrix products: 155 us -> none  [the longest x1 19.6 us: f(): b_p = jnp.dot(xs2, wu, preferred_element_type=f32).reshape(ny, nx, td, fc)]
    all_to_all x2 -> x0, blocking collectives: 31.5 us -> none  [to_cols(): return lax.all_to_all(t, 'dp', 0, 0, tiled=True)]
    unnamed x24 -> x0, local copies, waits for them, and re-layouts: 31.3 us -> none
  transfers between devices with their start and end apart: 9 -> 0, of which waited for: 6 -> 0; matrix products, arithmetic and copies ran while one was open for 10% -> 0% of each run, Pallas kernels for 0% -> 0%
where the time goes in v2:
time: 404 us; the launch traced here: 400 us
  Pallas kernels  400 us (99%)
    pallas_call x1, Pallas kernels, f(): pl.pallas_call(functools.partial(_kernel, z), out_shape=outs, in_specs=[h...  387 us
    pallas_call x1, Pallas kernels, _results(): pl.pallas_call(functools.partial(_move, pieces), out_shape=shapes + [like...  12.5 us

profile of v2, /device:TPU:97, one launch (start us, length us, event | category | flops | bytes accessed | tf_op | source)
XLA Modules:
  0.0 400.3 jit_solution(8243035450735307734)
XLA Ops:
  0.6 387.1 %mlp.1 = (bf16[64,5120]{1,0:T(8,128)(2,1)}, bf16[64,5120]{1,0:T(8,128)(2,1)}, f32[2,640,3584]{2,1,0:T(8,128)S(1)}, f32[3456,640]{1,0:T(8,128)}, bf16[2,4,4,64,51...) custom-call(bf16[64,5120]{1,0:T(8,128)(2,1)} %x_ref.1, ...), custom_call_target="tpu_custom_call" | custom-call | tf_op jit(solution)/shard_map/mlp/pallas_call | solution.py:989
  387.7 12.5 %results.1 = (bf16[64,5120]{1,0:T(8,128)(2,1)}, bf16[64,5120]{1,0:T(8,128)(2,1)}, f32[640,3456]{1,0:T(8,128)}, f32[640,3456]{1,0:T(8,128)}, f32[3456,640]{1,0:T(8,128)}) custom-call(bf16[64,5120]{1,0:T(8,128)(2,1)} %get-tuple-element.9.y, bf16[64,5120]{1,0:T(8,128)(2,1)} %get-tuple-element.10.dx, f32[2,640,3584]{2,1,0:T(8,128)S(1)} %get-tuple-element.11.dw, ...), custom_call_target="tpu_custom_call" | custom-call | tf_op jit(solution)/shard_map/results/pallas_call | solution.py:944

commit v3 on v2

--- a/solution.py
+++ b/solution.py
@@ -47,9 +47,9 @@
     return _dot(a, b, 1, 1)
 
 
-def _start(cps):
+def _start(cps, urgent=False):
     for cp in cps:
-        cp.start(priority=1)
+        cp.start(priority=0 if urgent else 1)
 
 
 def _wait(cps):
@@ -88,7 +88,7 @@
 def _kernel(z, x_ref, wg_ref, wu_ref, wd_ref, dy_ref,
             y_ref, dx_ref, dw, dwd_ref,
             xh, xp, wt, wdt, wsl, wmt, ha, dda, rsb,
-            xs, xr, ys, yr, ws, wr, ps, pr, es, er, ags, agr, rss, rsr, a2s, a2r):
+            xs, xr, ys, yr, ws, wr, ps, pr, es, er, ags, agr, rss, rsr, a2s, a2r, rsv):
     nc, ny, nj = z.nc, z.ny, z.nj
     ft, fc, dp, dc, mc, hc, td = z.ft, z.fc, z.dp, z.dc, z.mc, z.hc, z.td
     half, hn, last = td // 2, nc // 2, nj - 1
@@ -426,6 +426,9 @@
                 y_pass(DY, LEFT)
                 w_pass(UP, FAR)
                 y_pass(DY, FAR)
+            elif (w, o) == (DOWN, RIGHT):
+                w_pass(DOWN, LEFT)
+                w_pass(DOWN, RIGHT)
             elif o != OWN and (w == UP or o == FAR):
                 w_pass(w, o)
             w_got(w, o)
@@ -437,15 +440,13 @@
                 w_send(DOWN)
                 return
             hidden()
-            g_send(H, 0)
-            g_send(H, 1)
+            for j in range(3):
+                g_send(H, j)
             e_copy(X).start()
             for o in CHIPS:
                 y_last(DY, o)
-            w_pass(DOWN, LEFT)
-            w_pass(DOWN, RIGHT)
-
-        early = [(GATE, o) for o in CHIPS] + [(UP, LEFT), (DOWN, RIGHT), (DOWN, LEFT)]
+
+        early = [(GATE, o) for o in CHIPS] + [(UP, LEFT), (DOWN, LEFT)]
         products(before, early, after)
         e_copy(DY).start()
         grads()
@@ -495,7 +496,7 @@
 
         def share_start(q, j, o):
             share_blank(q, o % 2)
-            _start(share_load(q, j, o))
+            _start(share_load(q, j, o), True)
 
         def share(q, j, o, wc, u=None):
             _wait(share_load(q, j, o, u))
@@ -530,13 +531,10 @@
                 v = pt[p, _row(i * wide, wide), _lane(u * hc, hc)].T
                 pv[s, pl.ds(u * hn, hn), :, :, _lane(i * wide, wide)] = v.reshape(hn, ny, ROWS, wide)
 
-        def rs_copy(s, u, i):
-            r = i - 1
-            return rc(pv.at[s % 3, pl.ds(u * hn, hn), ty(i)], rsb.at[s, u, r], rss.at[s], rsr.at[s, u], dev(c, ty(i), k))
-
-        def rs_send(s, u):
+        def rs_send(s, u, dst=None):
             for i in range(1, ny):
-                rs_copy(s, u, i).start()
+                to = rsb.at[s, u, i - 1] if dst is None else dst.at[u, i - 1]
+                rc(pv.at[s % 3, pl.ds(u * hn, hn), ty(i)], to, rss.at[s], rsr.at[s, u], dev(c, ty(i), k)).start()
 
         def rs_free(s):
             left_for(pv.at[s % 3, :, pl.ds(0, ny - 1)], rss.at[s])
@@ -556,13 +554,18 @@
         def out_local(s, dst):
             return pltpu.make_async_copy(ov.at[s, c], dst, lsem.at[s])
 
+        def out_one(s, dst, cc):
+            @pl.when(cc != c)
+            def _():
+                out_copy(s, dst, cc).start()
+
+            @pl.when(cc == c)
+            def _():
+                _start([out_local(s, dst)], True)
+
         def out_send(q, j):
-            s, dst = at_of(q, j), out_rows(q, j)
             for cc in range(nc):
-                @pl.when(cc != c)
-                def _():
-                    out_copy(s, dst, cc).start()
-            _start([out_local(s, dst)])
+                out_one(at_of(q, j), out_rows(q, j), cc)
 
         def out_done(s):
             v = ov.at[s, pl.ds(0, nc - 1)]
@@ -570,30 +573,38 @@
             arrived(v, a2r, s, mate)
             out_local(s, out_rows(H, 0)).wait()
 
+        def residual(q, j, u):
+            rows = pl.ds(u * hn, hn)
+            return pltpu.make_async_copy(xh.at[q, rows, t, _row(j * ROWS, ROWS), _lane(c * dc, dc)], tv.at[rows],
+                                         fsem.at[1, u])
+
         def finish_loads(q, j, u):
-            rows = pl.ds(u * hn, hn)
-            return [pltpu.make_async_copy(rsb.at[at_of(q, j), u], rv.at[u], fsem.at[0, u]),
-                    pltpu.make_async_copy(xh.at[q, rows, t, _row(j * ROWS, ROWS), _lane(c * dc, dc)], tv.at[rows],
-                                          fsem.at[1, u])]
+            return [pltpu.make_async_copy(rsb.at[at_of(q, j), u], rv.at[u], fsem.at[0, u]), residual(q, j, u)]
 
         def finish_start(q, j):
             @pl.loop(0, two)
             def _(u):
                 arrived(rsb.at[at_of(q, j), u], rsr, (at_of(q, j), u), mate)
-                _start(finish_loads(q, j, u))
-
-        def finish(q, j):
+                _start(finish_loads(q, j, u), True)
+
+        def finish(q, j, late=None):
             s = at_of(q, j)
 
             @pl.loop(0, two)
             def _(u):
-                _wait(finish_loads(q, j, u))
+                if late is None:
+                    _wait(finish_loads(q, j, u))
+                else:
+                    arrived(late.at[u], rsr, (s, u), mate)
+                    residual(q, j, u).wait()
                 for i in range(hn):
                     cc = u * hn + i
                     tot = pv[s % 3, cc, t]
                     for m in range(ny - 1):
-                        tot = tot + rv[u, m, i]
+                        tot = tot + (rv if late is None else late)[u, m, i]
                     ov[s, cc] = (tv[cc].astype(F32) + tot).astype(BF16)
+                    if late is not None:
+                        out_one(s, out_rows(q, j), cc)
 
         def tok_load(a, j, buf, s):
             rows = _row(j * ROWS, ROWS)
@@ -605,7 +616,7 @@
             loads = wide_load(wc, wdt, wmt.at[DOWN], psem)
             _start(loads)
             g_pass(H, 0)
-            g_send(H, 2)
+            g_send(H, 3)
             blank(wc)
             _clear(acc)
             for w in PAIR:
@@ -641,13 +652,13 @@
                     g_pass(D, 0)
                     g_send(D, 2)
 
-                @pl.when(before & (j < nj - 2))
-                def _():
-                    g_send(H, j + 2)
-
-                @pl.when((j >= nj - 2) & here)
-                def _():
-                    g_send(D, j - (nj - 2))
+                @pl.when(j == 1)
+                def _():
+                    g_send(D, 0)
+
+                @pl.when(j == last)
+                def _():
+                    g_send(D, 1)
 
                 @pl.when(before)
                 def _():
@@ -846,6 +857,23 @@
             _start(d_load(last, near, (0,)))
             share(D, last, RIGHT, wc)
             share_blank(D, FAR % 2)
+            share(D, last, LEFT, wc)
+            g_last(D, last, 0)
+            _start(share_load(D, last, FAR, 0), True)
+
+            @pl.loop(0, two)
+            def _(u):
+                @pl.when(u == 1)
+                def _():
+                    g_last(D, last, 1)
+                    _start(share_load(D, last, FAR, 1), True)
+                share(D, last, FAR, wc, u)
+                upright(D, last, u)
+                rs_send(at_of(D, last), u, rsv)
+
+                @pl.when(u == 0)
+                def _():
+                    finish_start(D, m)
 
             @pl.loop(0, nj)
             def _(i):
@@ -854,23 +882,6 @@
             @pl.loop(0, m)
             def _(i):
                 out_send(D, i)
-            g_last(D, last, 0)
-            _start(share_load(D, last, FAR, 0))
-            share(D, last, LEFT, wc)
-
-            @pl.loop(0, two)
-            def _(u):
-                @pl.when(u == 1)
-                def _():
-                    g_last(D, last, 1)
-                    _start(share_load(D, last, FAR, 1))
-                share(D, last, FAR, wc, u)
-                upright(D, last, u)
-                rs_send(at_of(D, last), u)
-
-                @pl.when(u == 0)
-                def _():
-                    finish_start(D, m)
             for u in PAIR:
                 g_mate_near(D, last, u)
             _start(d_load(last, near, (1,)))
@@ -882,10 +893,9 @@
             for u in PAIR:
                 g_sent(D, last, u)
             _wait(d_load(last, CHIPS))
+            _start([residual(D, last, u) for u in PAIR], True)
             add_outer()
-            finish_start(D, last)
-            finish(D, last)
-            out_send(D, last)
+            finish(D, last, rsv)
             for i in range(3):
                 rs_free(nj + last - i)
 
@@ -991,7 +1001,8 @@
             out_shape=outs,
             in_specs=[hbm] * 5,
             out_specs=specs,
-            scratch_shapes=[sem(shape) for shape in shapes],
+            scratch_shapes=[sem(shape) for shape in shapes]
+            + [pltpu.VMEM((two, ny - 1, z.nc // 2, ROWS, z.dc), F32)],
             name="mlp",
             compiler_params=pltpu.CompilerParams(
                 collective_id=0, has_side_effects=True, vmem_limit_bytes=VMEM_LIMIT),

time: 404 us -> 398 us (0.985)
  Pallas kernels: 400 us -> 395 us
    pallas_call x1, Pallas kernels: 387 us -> 383 us  [f(): pl.pallas_call(functools.partial(_kernel, z), out_shape=outs, in_specs=[h...]
where the time goes in v3:
time: 398 us; the launch traced here: 396 us
  Pallas kernels  395 us (99%)
    pallas_call x1, Pallas kernels, f(): pl.pallas_call(functools.partial(_kernel, z), out_shape=outs, in_specs=[h...  383 us
    pallas_call x1, Pallas kernels, _results(): pl.pallas_call(functools.partial(_move, pieces), out_shape=shapes + [like...  12.5 us

profile of v3, /device:TPU:97, one launch (start us, length us, event | category | flops | bytes accessed | tf_op | source)
XLA Modules:
  0.0 395.8 jit_solution(799012164641740894)
XLA Ops:
  0.6 382.5 %mlp.1 = (bf16[64,5120]{1,0:T(8,128)(2,1)}, bf16[64,5120]{1,0:T(8,128)(2,1)}, f32[2,640,3584]{2,1,0:T(8,128)S(1)}, f32[3456,640]{1,0:T(8,128)}, bf16[2,4,4,64,51...) custom-call(bf16[64,5120]{1,0:T(8,128)(2,1)} %x_ref.1, ...), custom_call_target="tpu_custom_call" | custom-call | tf_op jit(solution)/shard_map/mlp/pallas_call | solution.py:999
  383.1 12.5 %results.1 = (bf16[64,5120]{1,0:T(8,128)(2,1)}, bf16[64,5120]{1,0:T(8,128)(2,1)}, f32[640,3456]{1,0:T(8,128)}, f32[640,3456]{1,0:T(8,128)}, f32[3456,640]{1,0:T(8,128)}) custom-call(bf16[64,5120]{1,0:T(8,128)(2,1)} %get-tuple-element.9.y, bf16[64,5120]{1,0:T(8,128)(2,1)} %get-tuple-element.10.dx, f32[2,640,3584]{2,1,0:T(8,128)S(1)} %get-tuple-element.11.dw, ...), custom_call_target="tpu_custom_call" | custom-call | tf_op jit(solution)/shard_map/results/pallas_call | solution.py:954

commit v4 on v3

--- a/solution.py
+++ b/solution.py
@@ -9,7 +9,7 @@
 
 F32, BF16 = jnp.float32, jnp.bfloat16
 LANES, ROWS = 128, 16
-VMEM_LIMIT = 48_000_000
+VMEM_LIMIT = 40_420_000
 X, DY = PAIR = range(2)
 GATE, UP, DOWN = WEIGHTS = range(3)
 H, D = range(2)
@@ -31,8 +31,12 @@
         self.hc = self.mc // 2
         starts = [c * self.ft for c in range(self.nc)]
         self.cover = -(-max(s % LANES + self.ft for s in starts) // LANES) * LANES
-        self.fp = max(s // LANES * LANES + self.cover for s in starts)
-        self.fw = -(-self.fc // (4 * LANES)) * 4 * LANES
+        self.back = max(s // LANES * LANES for s in starts) + self.cover - self.fc
+        tiles = self.fc // LANES
+        self.cuts = 3 if tiles % 3 == 0 else tiles
+
+    def under(self, cc):
+        return cc * self.ft // LANES * LANES - cc // (self.nc - 1) * self.back
 
 
 def _dot(a, b, ca, cb):
@@ -86,8 +90,8 @@
 
 
 def _kernel(z, x_ref, wg_ref, wu_ref, wd_ref, dy_ref,
-            y_ref, dx_ref, dw, dwd_ref,
-            xh, xp, wt, wdt, wsl, wmt, ha, dda, rsb,
+            y_ref, dx_ref, dw, dwd,
+            xh, xp, wt, wdt, wsl, wmt, ha, dda, rsb, ovh,
             xs, xr, ys, yr, ws, wr, ps, pr, es, er, ags, agr, rss, rsr, a2s, a2r, rsv):
     nc, ny, nj = z.nc, z.ny, z.nj
     ft, fc, dp, dc, mc, hc, td = z.ft, z.fc, z.dp, z.dc, z.mc, z.hc, z.td
@@ -256,7 +260,7 @@
             return pltpu.make_async_copy(xb.at[a], xh.at[a, c, t], bsem.at[1, a])
 
         def place(w):
-            return (tall.at[GATE], wide.at[GATE]) if w == DOWN else (wide.at[w], tall.at[w])
+            return (tall, wide) if w == DOWN else (wide, tall)
 
         def s_in(w):
             return pltpu.make_async_copy((wg_ref, wu_ref, wd_ref)[w], place(w)[0], tsem.at[0, w])
@@ -284,30 +288,27 @@
         x_send(X)
         y_send(X, OWN)
         x_send(DY)
-        for w in PAIR:
-            _start([s_in(w)])
-        for a in PAIR:
-            _start([x_in(a)])
-        for w in PAIR:
-            s_in(w).wait()
-            turned(w)
-        s_out(GATE).wait()
-        s_own(GATE).wait()
-        _start([s_in(DOWN)])
+        _start([s_in(GATE)] + [x_in(a) for a in PAIR])
+        s_in(GATE).wait()
+        turned(GATE)
+        _start([s_in(UP)])
         for a in PAIR:
             x_in(a).wait()
             _start([x_out(a)])
-        s_in(DOWN).wait()
-        turned(DOWN)
+        _wait([s_in(UP), s_out(GATE), s_own(GATE)])
+        turned(UP)
+        for w in WEIGHTS:
+            _clear(acc.at[w])
+        _wait([s_out(UP), s_own(UP)])
+        _start([s_in(DOWN)])
         x_pass(X)
         y_send(X, RIGHT)
         y_send(X, LEFT)
         for w in WEIGHTS:
-            _clear(acc.at[w])
-        for w in (UP, DOWN):
-            s_out(w).wait()
-        for w in WEIGHTS:
             w_mate(w)
+        s_in(DOWN).wait()
+        turned(DOWN)
+        s_out(DOWN).wait()
         x_pass(DY)
         x_last(X)
         y_send(X, FAR)
@@ -315,8 +316,7 @@
         for w in WEIGHTS:
             p_copy(w).start()
         x_last(DY)
-        for w in (UP, DOWN):
-            s_own(w).wait()
+        s_own(DOWN).wait()
         for a in PAIR:
             x_out(a).wait()
         for o in CHIPS:
@@ -457,8 +457,8 @@
         phase1,
         pltpu.VMEM((len(WEIGHTS), ft, nj * mc), F32),
         pltpu.VMEM((two, td, z.d), BF16),
-        pltpu.VMEM((two, dp, fc), BF16),
-        pltpu.VMEM((two, fc, dp), BF16),
+        pltpu.VMEM((dp, fc), BF16),
+        pltpu.VMEM((fc, dp), BF16),
         pltpu.VMEM((two, nj, nc, ny, ROWS, dc), BF16),
         pltpu.VMEM((two, ft, dc), BF16),
         pltpu.VMEM((nj, two, two, ft, hc), BF16),
@@ -468,17 +468,14 @@
     def at_of(q, j):
         return nj * q + j
 
-    def phase2(pt, pv, rv, tv, ov, sb, ssem, fsem, lsem):
+    def phase2(pt, pv, rv, tv, ov, sb, ssem, fsem, lsem, osem):
         def wide_load(dst, own, other, s):
-            return [pltpu.make_async_copy(v, dst.at[_row(kk * dp, dp), _head(fc)], s.at[i])
+            return [pltpu.make_async_copy(v, dst.at[_row(kk * dp, dp), :], s.at[i])
                     for i, (v, kk) in enumerate(zip((own, other), kinds))]
-
-        def blank(dst):
-            dst[:, fc:] = jnp.zeros((dc, z.fp - fc), BF16)
 
         def share_load(q, j, o, u=None):
             cc, slot = chip(o), o % 2
-            at = _row(cc * ft - cc * ft // LANES * LANES, ft)
+            at = _row(cc * ft - z.under(cc), ft)
             cps = []
             for i in range(1 + q):
                 for v in PAIR if u is None else (u,):
@@ -500,7 +497,7 @@
 
         def share(q, j, o, wc, u=None):
             _wait(share_load(q, j, o, u))
-            cols = _lane(chip(o) * ft // LANES * LANES, z.cover)
+            cols = _lane(z.under(chip(o)), z.cover)
             p = at_of(q, j) % 2
             at = _head(mc) if u is None else _lane(u * hc, hc)
             if q:
@@ -523,7 +520,7 @@
             shares(q, j, wc, OWN, FAR)
 
         def upright(q, j, u):
-            p, s = at_of(q, j) % 2, at_of(q, j) % 3
+            p = s = at_of(q, j) % 2
             wide = 2 * LANES
 
             @pl.loop(0, dc // wide)
@@ -534,12 +531,19 @@
         def rs_send(s, u, dst=None):
             for i in range(1, ny):
                 to = rsb.at[s, u, i - 1] if dst is None else dst.at[u, i - 1]
-                rc(pv.at[s % 3, pl.ds(u * hn, hn), ty(i)], to, rss.at[s], rsr.at[s, u], dev(c, ty(i), k)).start()
+                rc(pv.at[s % 2, pl.ds(u * hn, hn), ty(i)], to, rss.at[s], rsr.at[s, u], dev(c, ty(i), k)).start()
 
         def rs_free(s):
-            left_for(pv.at[s % 3, :, pl.ds(0, ny - 1)], rss.at[s])
+            left_for(pv.at[s % 2, :, pl.ds(0, ny - 1)], rss.at[s])
 
         def send_up(q, j):
+            if q:
+                rs_free(at_of(q, j) - 2)
+            else:
+                @pl.when(j > 1)
+                def _():
+                    rs_free(j - 2)
+
             @pl.loop(0, two)
             def _(u):
                 upright(q, j, u)
@@ -548,30 +552,28 @@
         def out_rows(q, j):
             return (dx_ref if q else y_ref).at[_row(j * ROWS, ROWS), _lane(c * dc, dc)]
 
-        def out_copy(s, dst, cc):
-            return rc(ov.at[s, cc], dst, a2s.at[s], a2r.at[s], dev(cc, t, k))
-
-        def out_local(s, dst):
-            return pltpu.make_async_copy(ov.at[s, c], dst, lsem.at[s])
-
-        def out_one(s, dst, cc):
+        def out_one(s, rows, dst, cc):
             @pl.when(cc != c)
             def _():
-                out_copy(s, dst, cc).start()
+                rc(rows.at[cc], dst, a2s.at[s], a2r.at[s], dev(cc, t, k)).start()
 
             @pl.when(cc == c)
             def _():
-                _start([out_local(s, dst)], True)
+                _start([pltpu.make_async_copy(rows.at[cc], dst, lsem.at[s])], True)
 
         def out_send(q, j):
+            s = at_of(q, j)
             for cc in range(nc):
-                out_one(at_of(q, j), out_rows(q, j), cc)
+                out_one(s, ovh.at[s], out_rows(q, j), cc)
 
         def out_done(s):
-            v = ov.at[s, pl.ds(0, nc - 1)]
+            v = ovh.at[s, _head(nc - 1)]
             left_for(v, a2s.at[s])
             arrived(v, a2r, s, mate)
-            out_local(s, out_rows(H, 0)).wait()
+            pltpu.make_async_copy(ovh.at[s, c], out_rows(H, 0), lsem.at[s]).wait()
+
+        def stored(s):
+            return pltpu.make_async_copy(ov.at[s % 2], ovh.at[s], osem.at[s % 2])
 
         def residual(q, j, u):
             rows = pl.ds(u * hn, hn)
@@ -599,26 +601,28 @@
                     residual(q, j, u).wait()
                 for i in range(hn):
                     cc = u * hn + i
-                    tot = pv[s % 3, cc, t]
+                    tot = pv[s % 2, cc, t]
                     for m in range(ny - 1):
                         tot = tot + (rv if late is None else late)[u, m, i]
-                    ov[s, cc] = (tv[cc].astype(F32) + tot).astype(BF16)
+                    ov[s % 2, cc] = (tv[cc].astype(F32) + tot).astype(BF16)
                     if late is not None:
-                        out_one(s, out_rows(q, j), cc)
+                        out_one(s, ov.at[s % 2], out_rows(q, j), cc)
+
+            if late is None:
+                _start([stored(s)])
 
         def tok_load(a, j, buf, s):
             rows = _row(j * ROWS, ROWS)
             return [pltpu.make_async_copy(xh.at[a, :, :, rows, _lane(me * dp, dp)], buf.at[0], s.at[0]),
                     pltpu.make_async_copy(xp.at[a, :, :, rows, :], buf.at[1], s.at[1])]
 
-        def phase2h(acc, wc, hv, kv, psem, dsem, ksem):
+        def phase2h(wc, hv, kv, psem, dsem, ksem):
             p_copy(DOWN).wait_recv()
             loads = wide_load(wc, wdt, wmt.at[DOWN], psem)
             _start(loads)
             g_pass(H, 0)
             g_send(H, 3)
-            blank(wc)
-            _clear(acc)
+            _clear(dwd)
             for w in PAIR:
                 p_copy(w).wait_recv()
                 e_copy(w).wait_recv()
@@ -634,7 +638,7 @@
                 @pl.loop(first, end)
                 def _(o):
                     rows = _row(chip(o) * ft, ft)
-                    acc[rows, :] += _nn(hv[rows, :], kv[...].reshape(2 * mc, dp))
+                    dwd[rows, :] += _nn(hv[rows, :], kv[...].reshape(2 * mc, dp))
 
             near = (OWN, RIGHT, LEFT)
             share_start(H, 0, OWN)
@@ -665,10 +669,6 @@
                     g_mate_near(H, j - 1)
                     _start(tok_load(DY, j - 1, kv, ksem))
                     _start(h_load(j - 1, near))
-
-                @pl.when((j >= 3) & here)
-                def _():
-                    rs_free(j - 3)
 
                 @pl.when(here)
                 def _():
@@ -707,18 +707,17 @@
                     _wait(h_load(j - 1, (FAR,)))
                     add_outer(FAR, FAR + 1)
 
+                @pl.when(j > 3)
+                def _():
+                    stored(j - 4).wait()
+
                 @pl.when(two_before)
                 def _():
                     finish(H, j - 2)
-
-            out = pltpu.make_async_copy(acc, dwd_ref, psem.at[0])
-            _start([out])
-            out.wait()
 
         pl.run_scoped(
             phase2h,
-            pltpu.VMEM((fc, dp), F32),
-            pltpu.VMEM((dc, z.fp), BF16),
+            pltpu.VMEM((dc, fc), BF16),
             pltpu.VMEM((fc, 2 * mc), BF16),
             pltpu.VMEM((two, nc, ny, ROWS, dp), BF16),
             sem((two,)), sem((two, len(CHIPS), two)), sem((two,)),
@@ -728,9 +727,7 @@
             loads = [cp for w in PAIR for cp in wide_load(wc.at[w], (wg_ref, wu_ref)[w], wmt.at[w], wsem.at[w])]
             _start(loads)
             for w in PAIR:
-                blank(wc.at[w])
                 _clear(dw.at[w])
-            dv[:, fc:] = jnp.zeros((two, z.fw - fc, 2 * mc), BF16)
             _wait(loads)
 
             def d_load(j, os, hs=PAIR, us=PAIR):
@@ -740,11 +737,11 @@
                         for i in hs for o in os for q in PAIR for u in us]
 
             def add_outer():
-                n = z.fw // 2
-
-                @pl.loop(0, 2 * two)
+                n = fc // z.cuts
+
+                @pl.loop(0, z.cuts * two)
                 def _(i):
-                    q, cols = i // 2, _lane(i % 2 * n, n)
+                    q, cols = i // z.cuts, _lane(i % z.cuts * n, n)
                     dw[q, :, cols] += _nt(kt[...], dv[q, cols, :])
 
             def far(j, us=(None,)):
@@ -798,7 +795,6 @@
                 def _():
                     near_start(j - 1)
 
-                rs_free(nj + j - 3)
                 front(D, j, wc)
 
                 @pl.when(before)
@@ -826,6 +822,10 @@
                     _wait(d_load(j - 1, CHIPS))
                     add_outer()
 
+                @pl.when(before)
+                def _():
+                    stored(nj + j - 4).wait()
+
                 @pl.when(first)
                 def _():
                     finish(H, last)
@@ -837,26 +837,27 @@
             m = last - 1
             near_start(m)
             back(m)
-            rs_free(nj + last - 3)
             _clear(pt.at[at_of(D, last) % 2])
             shares(D, m, wc, FAR, FAR + 1)
             send_up(D, m)
             finish_start(D, m - 1)
             far(m)
             shares(D, last, wc, OWN, RIGHT)
+            g_pass(D, last, 0)
             _wait(d_load(m, CHIPS))
             add_outer()
+            stored(nj + m - 3).wait()
             finish(D, m - 1)
             for i in range(m):
                 g_sent(D, i)
             _start(tok_load(X, last, kv, ksem))
-            for u in PAIR:
-                g_pass(D, last, u)
+            g_pass(D, last, 1)
             share_start(D, last, RIGHT)
             share_start(D, last, LEFT)
             _start(d_load(last, near, (0,)))
             share(D, last, RIGHT, wc)
             share_blank(D, FAR % 2)
+            rs_free(at_of(D, last) - 2)
             share(D, last, LEFT, wc)
             g_last(D, last, 0)
             _start(share_load(D, last, FAR, 0), True)
@@ -867,6 +868,16 @@
                 def _():
                     g_last(D, last, 1)
                     _start(share_load(D, last, FAR, 1), True)
+                    for i in PAIR:
+                        stored(nj + m - 2 + i).wait()
+
+                    @pl.loop(0, nj)
+                    def _(i):
+                        out_send(H, i)
+
+                    @pl.loop(0, m)
+                    def _(i):
+                        out_send(D, i)
                 share(D, last, FAR, wc, u)
                 upright(D, last, u)
                 rs_send(at_of(D, last), u, rsv)
@@ -874,20 +885,11 @@
                 @pl.when(u == 0)
                 def _():
                     finish_start(D, m)
-
-            @pl.loop(0, nj)
-            def _(i):
-                out_send(H, i)
-
-            @pl.loop(0, m)
-            def _(i):
-                out_send(D, i)
             for u in PAIR:
                 g_mate_near(D, last, u)
             _start(d_load(last, near, (1,)))
             _start(d_load(last, (FAR,), (0,)))
             finish(D, m)
-            out_send(D, m)
             far(last, PAIR)
             g_sent(D, m)
             for u in PAIR:
@@ -895,8 +897,10 @@
             _wait(d_load(last, CHIPS))
             _start([residual(D, last, u) for u in PAIR], True)
             add_outer()
+            stored(nj + m).wait()
+            out_send(D, m)
             finish(D, last, rsv)
-            for i in range(3):
+            for i in PAIR:
                 rs_free(nj + last - i)
 
             @pl.loop(0, 2 * nj)
@@ -905,8 +909,8 @@
 
         pl.run_scoped(
             phase2d,
-            pltpu.VMEM((two, dc, z.fp), BF16),
-            pltpu.VMEM((two, z.fw, 2 * mc), BF16),
+            pltpu.VMEM((two, dc, fc), BF16),
+            pltpu.VMEM((two, fc, 2 * mc), BF16),
             pltpu.VMEM((two, nc, ny, ROWS, dp), BF16),
             pltpu.VMEM((dp, 2 * mc), BF16),
             sem((two, two)), sem((two, len(CHIPS), two, two)), sem((two,)),
@@ -915,53 +919,44 @@
     pl.run_scoped(
         phase2,
         pltpu.VMEM((two, dc, mc), F32),
-        pltpu.VMEM((3, nc, ny, ROWS, dc), F32),
+        pltpu.VMEM((two, nc, ny, ROWS, dc), F32),
         pltpu.VMEM((two, ny - 1, hn, ROWS, dc), F32),
         pltpu.VMEM((nc, ROWS, dc), BF16),
-        pltpu.VMEM((2 * nj, nc, ROWS, dc), BF16),
+        pltpu.VMEM((two, nc, ROWS, dc), BF16),
         pltpu.VMEM((two, two, z.cover, mc), BF16),
-        sem((two, two, two)), sem((two, two)), sem((2 * nj,)),
+        sem((two, two, two)), sem((two, two)), sem((2 * nj,)), sem((two,)),
     )
 
 
-def _move(pieces, y, dx, dw, dwd, y_out, dx_out, dwg_out, dwu_out, dwd_out, y_buf, dx_buf, dwd_buf, sems):
-    small = [(a, b, o, 1) for a, b, o in ((y, y_buf, y_out), (dx, dx_buf, dx_out))]
-    moves = []
-    for a, b, o, n in [(dwd, dwd_buf, dwd_out, pieces)] + small:
-        rows = a.shape[0] // n
-        moves += [[x.at[pl.ds(i * rows, rows)] for x in (a, b, o)] for i in range(n)]
-
-    def copy(i, leg):
-        return pltpu.make_async_copy(moves[i][leg], moves[i][leg + 1], sems.at[leg, i])
-
-    direct = [pltpu.make_async_copy(dw.at[q, :, _head(o.shape[1])], o, sems.at[0, len(moves) + q])
-              for q, o in enumerate((dwg_out, dwu_out))]
-    for i in range(len(moves)):
-        copy(i, 0).start()
-    _start(direct)
-    for i in range(len(moves)):
-        copy(i, 0).wait()
-        copy(i, 1).start()
-    for i in range(len(moves)):
-        copy(i, 1).wait()
-    _wait(direct)
-
-
-def _results(y, dx, dw, dwd, like, pieces):
-    hbm, vmem = (pl.BlockSpec(memory_space=m) for m in (pltpu.HBM, pltpu.VMEM))
+def _move(y, dx, dw, dwd, y_out, dx_out, dwg_out, dwu_out, dwd_out, bufs, sems):
+    rows = [(y, bufs.at[0], y_out), (dx, bufs.at[1], dx_out)]
+    grads = [(dwd, dwd_out)] + [(dw.at[q], o) for q, o in enumerate((dwg_out, dwu_out))]
+    read = [pltpu.make_async_copy(a, b, sems.at[i]) for i, (a, b, _) in enumerate(rows)]
+    write = [pltpu.make_async_copy(b, o, sems.at[i]) for i, (_, b, o) in enumerate(rows)]
+    out = [pltpu.make_async_copy(a, o, sems.at[len(rows) + i]) for i, (a, o) in enumerate(grads)]
+    _start(read, True)
+    _start(out)
+    for a, b in zip(read, write):
+        a.wait()
+        _start([b], True)
+    _wait(write + out)
+
+
+def _results(y, dx, dw, dwd, like):
+    hbm, vmem = pltpu.HBM, pltpu.VMEM
+    spaces = (hbm, hbm, vmem, vmem)
     like = jax.ShapeDtypeStruct(like.shape, F32)
-    shapes = [jax.ShapeDtypeStruct(a.shape, a.dtype) for a in (y, dx)]
+    rows = [jax.ShapeDtypeStruct(a.shape, a.dtype) for a in (y, dx)]
+    outs = rows + [like, like, jax.ShapeDtypeStruct(dwd.shape, F32)]
     return pl.pallas_call(
-        functools.partial(_move, pieces),
-        out_shape=shapes + [like, like, jax.ShapeDtypeStruct(dwd.shape, F32)],
-        in_specs=[hbm, hbm, vmem, hbm],
-        out_specs=[hbm] * 5,
-        scratch_shapes=[pltpu.VMEM(a.shape, a.dtype) for a in (y, dx, dwd)]
-        + [pltpu.SemaphoreType.DMA((2, pieces + 4))],
+        _move,
+        out_shape=outs,
+        in_specs=[pl.BlockSpec(memory_space=m) for m in spaces],
+        out_specs=[pl.BlockSpec(memory_space=hbm)] * len(outs),
+        scratch_shapes=[vmem((len(rows), *y.shape), y.dtype), pltpu.SemaphoreType.DMA((len(outs),))],
         name="results",
-        compiler_params=pltpu.CompilerParams(vmem_limit_bytes=VMEM_LIMIT // 2),
-    )(*(pltpu.with_memory_space_constraint(v, m)
-        for v, m in ((y, pltpu.HBM), (dx, pltpu.HBM), (dw, pltpu.VMEM), (dwd, pltpu.HBM))))
+        compiler_params=pltpu.CompilerParams(vmem_limit_bytes=VMEM_LIMIT // 10),
+    )(*(pltpu.with_memory_space_constraint(v, m) for v, m in zip((y, dx, dw, dwd), spaces)))
 
 
 def solution(mesh):
@@ -979,7 +974,7 @@
         bf16 = functools.partial(jax.ShapeDtypeStruct, dtype=BF16)
         f32 = functools.partial(jax.ShapeDtypeStruct, dtype=F32)
         outs = [
-            bf16(x.shape), bf16(x.shape), pltpu.VMEM((two, z.dp, z.fw), F32), f32(wd.shape),
+            bf16(x.shape), bf16(x.shape), pltpu.VMEM((two, z.dp, z.fc), F32), pltpu.VMEM(wd.shape, F32),
             bf16((two, z.nc, ny, z.td, z.d)),
             bf16((two, z.nc, ny, z.td, z.dp)),
             bf16((two, z.fc, z.dp)),
@@ -989,9 +984,10 @@
             bf16((z.nj, two, z.nc, two, z.ft, z.hc)),
             bf16((z.nj, two, z.nc, two, two, z.ft, z.hc)),
             f32((steps, two, ny - 1, z.nc // 2, ROWS, z.dc)),
+            bf16((steps, z.nc, ROWS, z.dc)),
         ]
         specs = [hbm] * len(outs)
-        specs[2] = vmem
+        specs[2:4] = [vmem] * 2
         sem = pltpu.SemaphoreType.DMA
         chips = len(CHIPS)
         shapes = ((two,), (two, 3), (two,), (two, chips, 3), (kinds,), (kinds, chips), (kinds,), (kinds, chips),
@@ -1007,7 +1003,7 @@
             compiler_params=pltpu.CompilerParams(
                 collective_id=0, has_side_effects=True, vmem_limit_bytes=VMEM_LIMIT),
         )(x, wg, wu, wd, dy)
-        return tuple(_results(*r[:4], wg, 8))
+        return tuple(_results(*r[:4], wg))
 
     return jax.shard_map(f, mesh=mesh, in_specs=(row_spec, win_spec, win_spec, wout_spec, row_spec),
                          out_specs=(row_spec, row_spec, win_spec, win_spec, wout_spec), check_vma=False)

time: 398 us -> 395 us (level)
  no operation moved by 1% of the time
where the time goes in v4:
time: 395 us; the launch traced here: 393 us
  Pallas kernels  392 us (99%)
    pallas_call x1, Pallas kernels, f(): pl.pallas_call(functools.partial(_kernel, z), out_shape=outs, in_specs=[h...  382 us
    pallas_call x1, Pallas kernels, _results(): pl.pallas_call(_move, out_shape=outs, in_specs=[pl.BlockSpec(memory_space...  9.56 us

profile of v4, /device:TPU:97, one launch (start us, length us, event | category | flops | bytes accessed | tf_op | source)
XLA Modules:
  0.0 392.6 jit_solution(18312449389177420077)
XLA Ops:
  0.6 382.2 %mlp.1 = (bf16[64,5120]{1,0:T(8,128)(2,1)}, bf16[64,5120]{1,0:T(8,128)(2,1)}, f32[2,640,3456]{2,1,0:T(8,128)S(1)}, f32[3456,640]{1,0:T(8,128)S(1)}, bf16[2,4,4,6...) custom-call(bf16[64,5120]{1,0:T(8,128)(2,1)} %x_ref.1, ...), custom_call_target="tpu_custom_call" | custom-call | tf_op jit(solution)/shard_map/mlp/pallas_call | solution.py:995
  382.9 9.6 %results.1 = (bf16[64,5120]{1,0:T(8,128)(2,1)}, bf16[64,5120]{1,0:T(8,128)(2,1)}, f32[640,3456]{1,0:T(8,128)}, f32[640,3456]{1,0:T(8,128)}, f32[3456,640]{1,0:T(8,128)}) custom-call(bf16[64,5120]{1,0:T(8,128)(2,1)} %get-tuple-element.9.y, bf16[64,5120]{1,0:T(8,128)(2,1)} %get-tuple-element.10.dx, f32[2,640,3456]{2,1,0:T(8,128)S(1)} %get-tuple-element.11.dw, ...), custom_call_target="tpu_custom_call" | custom-call | tf_op jit(solution)/shard_map/results/pallas_call | solution.py:951

commit v5 on v4

--- a/solution.py
+++ b/solution.py
@@ -529,7 +529,9 @@
                 pv[s, pl.ds(u * hn, hn), :, :, _lane(i * wide, wide)] = v.reshape(hn, ny, ROWS, wide)
 
         def rs_send(s, u, dst=None):
-            for i in range(1, ny):
+            near_first = list(range(1, ny))
+            far_first = sorted(near_first, key=lambda i: -min(i, ny - i))
+            for i in near_first if dst is None else far_first:
                 to = rsb.at[s, u, i - 1] if dst is None else dst.at[u, i - 1]
                 rc(pv.at[s % 2, pl.ds(u * hn, hn), ty(i)], to, rss.at[s], rsr.at[s, u], dev(c, ty(i), k)).start()
 
@@ -840,12 +842,12 @@
             _clear(pt.at[at_of(D, last) % 2])
             shares(D, m, wc, FAR, FAR + 1)
             send_up(D, m)
-            finish_start(D, m - 1)
             far(m)
             shares(D, last, wc, OWN, RIGHT)
             g_pass(D, last, 0)
             _wait(d_load(m, CHIPS))
             add_outer()
+            finish_start(D, m - 1)
             stored(nj + m - 3).wait()
             finish(D, m - 1)
             for i in range(m):
@@ -928,32 +930,37 @@
     )
 
 
-def _move(y, dx, dw, dwd, y_out, dx_out, dwg_out, dwu_out, dwd_out, bufs, sems):
+def _move(cuts, y, dx, dw, dwd, y_out, dx_out, dwg_out, dwu_out, dwd_out, bufs, sems):
     rows = [(y, bufs.at[0], y_out), (dx, bufs.at[1], dx_out)]
     grads = [(dwd, dwd_out)] + [(dw.at[q], o) for q, o in enumerate((dwg_out, dwu_out))]
     read = [pltpu.make_async_copy(a, b, sems.at[i]) for i, (a, b, _) in enumerate(rows)]
     write = [pltpu.make_async_copy(b, o, sems.at[i]) for i, (_, b, o) in enumerate(rows)]
-    out = [pltpu.make_async_copy(a, o, sems.at[len(rows) + i]) for i, (a, o) in enumerate(grads)]
+    out = []
+    for r in range(cuts):
+        for a, o in grads:
+            n = a.shape[0] // cuts
+            out.append(pltpu.make_async_copy(a.at[_half(r, n)], o.at[_half(r, n)], sems.at[len(rows) + len(out)]))
     _start(read, True)
-    _start(out)
+    for i in PAIR:
+        _start(out[i::2], i == 1)
     for a, b in zip(read, write):
         a.wait()
         _start([b], True)
     _wait(write + out)
 
 
-def _results(y, dx, dw, dwd, like):
+def _results(y, dx, dw, dwd, like, cuts):
     hbm, vmem = pltpu.HBM, pltpu.VMEM
     spaces = (hbm, hbm, vmem, vmem)
     like = jax.ShapeDtypeStruct(like.shape, F32)
     rows = [jax.ShapeDtypeStruct(a.shape, a.dtype) for a in (y, dx)]
     outs = rows + [like, like, jax.ShapeDtypeStruct(dwd.shape, F32)]
     return pl.pallas_call(
-        _move,
+        functools.partial(_move, cuts),
         out_shape=outs,
         in_specs=[pl.BlockSpec(memory_space=m) for m in spaces],
         out_specs=[pl.BlockSpec(memory_space=hbm)] * len(outs),
-        scratch_shapes=[vmem((len(rows), *y.shape), y.dtype), pltpu.SemaphoreType.DMA((len(outs),))],
+        scratch_shapes=[vmem((len(rows), *y.shape), y.dtype), pltpu.SemaphoreType.DMA((len(rows) + 3 * cuts,))],
         name="results",
         compiler_params=pltpu.CompilerParams(vmem_limit_bytes=VMEM_LIMIT // 10),
     )(*(pltpu.with_memory_space_constraint(v, m) for v, m in zip((y, dx, dw, dwd), spaces)))
@@ -1003,7 +1010,7 @@
             compiler_params=pltpu.CompilerParams(
                 collective_id=0, has_side_effects=True, vmem_limit_bytes=VMEM_LIMIT),
         )(x, wg, wu, wd, dy)
-        return tuple(_results(*r[:4], wg))
+        return tuple(_results(*r[:4], wg, 4))
 
     return jax.shard_map(f, mesh=mesh, in_specs=(row_spec, win_spec, win_spec, wout_spec, row_spec),
                          out_specs=(row_spec, row_spec, win_spec, win_spec, wout_spec), check_vma=False)

time: 395 us -> 394 us (level)
  no operation moved by 1% of the time
where the time goes in v5:
time: 394 us; the launch traced here: 393 us
  Pallas kernels  393 us (100%)
    pallas_call x1, Pallas kernels, f(): pl.pallas_call(functools.partial(_kernel, z), out_shape=outs, in_specs=[h...  383 us
    pallas_call x1, Pallas kernels, _results(): pl.pallas_call(functools.partial(_move, cuts), out_shape=outs, in_specs=[...  9.32 us

profile of v5, /device:TPU:97, one launch (start us, length us, event | category | flops | bytes accessed | tf_op | source)
XLA Modules:
  0.0 393.4 jit_solution(12990966652377661509)
XLA Ops:
  0.6 383.3 %mlp.1 = (bf16[64,5120]{1,0:T(8,128)(2,1)}, bf16[64,5120]{1,0:T(8,128)(2,1)}, f32[2,640,3456]{2,1,0:T(8,128)S(1)}, f32[3456,640]{1,0:T(8,128)S(1)}, bf16[2,4,4,6...) custom-call(bf16[64,5120]{1,0:T(8,128)(2,1)} %x_ref.1, ...), custom_call_target="tpu_custom_call" | custom-call | tf_op jit(solution)/shard_map/mlp/pallas_call | solution.py:1002
  384.0 9.3 %results.1 = (bf16[64,5120]{1,0:T(8,128)(2,1)}, bf16[64,5120]{1,0:T(8,128)(2,1)}, f32[640,3456]{1,0:T(8,128)}, f32[640,3456]{1,0:T(8,128)}, f32[3456,640]{1,0:T(8,128)}) custom-call(bf16[64,5120]{1,0:T(8,128)(2,1)} %get-tuple-element.9.y, bf16[64,5120]{1,0:T(8,128)(2,1)} %get-tuple-element.10.dx, f32[2,640,3456]{2,1,0:T(8,128)S(1)} %get-tuple-element.11.dw, ...), custom_call_target="tpu_custom_call" | custom-call | tf_op jit(solution)/shard_map/results/pallas_call | solution.py:958

commit v6 on v5

--- a/solution.py
+++ b/solution.py
@@ -533,10 +533,10 @@
             far_first = sorted(near_first, key=lambda i: -min(i, ny - i))
             for i in near_first if dst is None else far_first:
                 to = rsb.at[s, u, i - 1] if dst is None else dst.at[u, i - 1]
-                rc(pv.at[s % 2, pl.ds(u * hn, hn), ty(i)], to, rss.at[s], rsr.at[s, u], dev(c, ty(i), k)).start()
+                rc(pv.at[s % 2, pl.ds(u * hn, hn), ty(i)], to, rss.at[s % 2], rsr.at[s, u], dev(c, ty(i), k)).start()
 
         def rs_free(s):
-            left_for(pv.at[s % 2, :, pl.ds(0, ny - 1)], rss.at[s])
+            left_for(pv.at[s % 2, :, pl.ds(0, ny - 1)], rss.at[s % 2])
 
         def send_up(q, j):
             if q:
@@ -557,7 +557,7 @@
         def out_one(s, rows, dst, cc):
             @pl.when(cc != c)
             def _():
-                rc(rows.at[cc], dst, a2s.at[s], a2r.at[s], dev(cc, t, k)).start()
+                rc(rows.at[cc], dst, a2s.at[0], a2r.at[0], dev(cc, t, k)).start()
 
             @pl.when(cc == c)
             def _():
@@ -569,9 +569,6 @@
                 out_one(s, ovh.at[s], out_rows(q, j), cc)
 
         def out_done(s):
-            v = ovh.at[s, _head(nc - 1)]
-            left_for(v, a2s.at[s])
-            arrived(v, a2r, s, mate)
             pltpu.make_async_copy(ovh.at[s, c], out_rows(H, 0), lsem.at[s]).wait()
 
         def stored(s):
@@ -633,7 +630,7 @@
             def h_load(j, os, hs=PAIR):
                 return [pltpu.make_async_copy(ha.at[j, kinds[i], cx(STEPS[o]), u],
                                               hv.at[_row(cx(STEPS[o]) * ft, ft), pl.ds(i * mc + u * hc, hc)],
-                                              dsem.at[i, o, u])
+                                              dsem.at[o // FAR])
                         for i in hs for o in os for u in PAIR]
 
             def add_outer(first, end):
@@ -642,6 +639,10 @@
                     rows = _row(chip(o) * ft, ft)
                     dwd[rows, :] += _nn(hv[rows, :], kv[...].reshape(2 * mc, dp))
 
+            def all_read(j, first, n):
+                v = ha.at[j, :, _head(n)]
+                pltpu.make_async_copy(v, v, dsem.at[first // FAR]).wait()
+
             near = (OWN, RIGHT, LEFT)
             share_start(H, 0, OWN)
 
@@ -693,7 +694,7 @@
                 @pl.when(before)
                 def _():
                     _wait(tok_load(DY, j - 1, kv, ksem))
-                    _wait(h_load(j - 1, near))
+                    all_read(j - 1, OWN, FAR)
                     add_outer(OWN, FAR)
                     shares(H, j - 1, wc, FAR, FAR + 1)
                     g_mate_far(H, j - 1)
@@ -706,7 +707,7 @@
 
                 @pl.when(before)
                 def _():
-                    _wait(h_load(j - 1, (FAR,)))
+                    all_read(j - 1, FAR, 1)
                     add_outer(FAR, FAR + 1)
 
                 @pl.when(j > 3)
@@ -722,7 +723,7 @@
             pltpu.VMEM((dc, fc), BF16),
             pltpu.VMEM((fc, 2 * mc), BF16),
             pltpu.VMEM((two, nc, ny, ROWS, dp), BF16),
-            sem((two,)), sem((two, len(CHIPS), two)), sem((two,)),
+            sem((two,)), sem((two,)), sem((two,)),
         )
 
         def phase2d(wc, dv, kv, kt, wsem, dsem, ksem):
@@ -735,8 +736,11 @@
             def d_load(j, os, hs=PAIR, us=PAIR):
                 return [pltpu.make_async_copy(dda.at[j, kinds[i], cx(STEPS[o]), q, u],
                                               dv.at[q, _row(cx(STEPS[o]) * ft, ft), pl.ds(i * mc + u * hc, hc)],
-                                              dsem.at[i, o, q, u])
+                                              dsem.at[0])
                         for i in hs for o in os for q in PAIR for u in us]
+
+            def all_read(j):
+                pltpu.make_async_copy(dda.at[j], dda.at[j], dsem.at[0]).wait()
 
             def add_outer():
                 n = fc // z.cuts
@@ -821,7 +825,7 @@
                 @pl.when(before)
                 def _():
                     far(j - 1)
-                    _wait(d_load(j - 1, CHIPS))
+                    all_read(j - 1)
                     add_outer()
 
                 @pl.when(before)
@@ -845,7 +849,7 @@
             far(m)
             shares(D, last, wc, OWN, RIGHT)
             g_pass(D, last, 0)
-            _wait(d_load(m, CHIPS))
+            all_read(m)
             add_outer()
             finish_start(D, m - 1)
             stored(nj + m - 3).wait()
@@ -896,7 +900,7 @@
             g_sent(D, m)
             for u in PAIR:
                 g_sent(D, last, u)
-            _wait(d_load(last, CHIPS))
+            all_read(last)
             _start([residual(D, last, u) for u in PAIR], True)
             add_outer()
             stored(nj + m).wait()
@@ -905,9 +909,13 @@
             for i in PAIR:
                 rs_free(nj + last - i)
 
+            v = ovh.at[:, _head(nc - 1)]
+            left_for(v, a2s.at[0])
+
             @pl.loop(0, 2 * nj)
             def _(i):
                 out_done(i)
+            arrived(v, a2r, 0, mate)
 
         pl.run_scoped(
             phase2d,
@@ -915,7 +923,7 @@
             pltpu.VMEM((two, fc, 2 * mc), BF16),
             pltpu.VMEM((two, nc, ny, ROWS, dp), BF16),
             pltpu.VMEM((dp, 2 * mc), BF16),
-            sem((two, two)), sem((two, len(CHIPS), two, two)), sem((two,)),
+            sem((two, two)), sem((1,)), sem((two,)),
         )
 
     pl.run_scoped(
@@ -998,7 +1006,7 @@
         sem = pltpu.SemaphoreType.DMA
         chips = len(CHIPS)
         shapes = ((two,), (two, 3), (two,), (two, chips, 3), (kinds,), (kinds, chips), (kinds,), (kinds, chips),
-                  (two,), (two + kinds,), (steps + 1, two), (steps + 1, 5), (steps,), (steps, two), (steps,), (steps,))
+                  (two,), (two + kinds,), (steps + 1, two), (steps + 1, 5), (two,), (steps, two), (1,), (1,))
         r = pl.pallas_call(
             functools.partial(_kernel, z),
             out_shape=outs,

time: 394 us -> 394 us (level)
  no operation moved by 1% of the time
where the time goes in v6:
time: 394 us; the launch traced here: 393 us
  Pallas kernels  392 us (99%)
    pallas_call x1, Pallas kernels, f(): pl.pallas_call(functools.partial(_kernel, z), out_shape=outs, in_specs=[h...  383 us
    pallas_call x1, Pallas kernels, _results(): pl.pallas_call(functools.partial(_move, cuts), out_shape=outs, in_specs=[...  9.32 us

profile of v6, /device:TPU:97, one launch (start us, length us, event | category | flops | bytes accessed | tf_op | source)
XLA Modules:
  0.0 393.3 jit_solution(17274250561034902661)
XLA Ops:
  0.6 383.1 %mlp.1 = (bf16[64,5120]{1,0:T(8,128)(2,1)}, bf16[64,5120]{1,0:T(8,128)(2,1)}, f32[2,640,3456]{2,1,0:T(8,128)S(1)}, f32[3456,640]{1,0:T(8,128)S(1)}, bf16[2,4,4,6...) custom-call(bf16[64,5120]{1,0:T(8,128)(2,1)} %x_ref.1, ...), custom_call_target="tpu_custom_call" | custom-call | tf_op jit(solution)/shard_map/mlp/pallas_call | solution.py:1010
  383.8 9.3 %results.1 = (bf16[64,5120]{1,0:T(8,128)(2,1)}, bf16[64,5120]{1,0:T(8,128)(2,1)}, f32[640,3456]{1,0:T(8,128)}, f32[640,3456]{1,0:T(8,128)}, f32[3456,640]{1,0:T(8,128)}) custom-call(bf16[64,5120]{1,0:T(8,128)(2,1)} %get-tuple-element.9.y, bf16[64,5120]{1,0:T(8,128)(2,1)} %get-tuple-element.10.dx, f32[2,640,3456]{2,1,0:T(8,128)S(1)} %get-tuple-element.11.dw, ...), custom_call_target="tpu_custom_call" | custom-call | tf_op jit(solution)/shard_map/results/pallas_call | solution.py:966
